TPU v7x, 32 devices: a whole 2x2x4 slice. The times are simulated.
32 devices in a mesh: prow: 4 (over x, core), pcol: 8 (over z, y).
Axes of the slice: x: 2, y: 2, z: 4, core: 2. Of those that a mesh axis runs over, the one named last changes fastest.
Arguments:
- child_u: bfloat16 [2, 10, 4, 2, 8, 512, 128], P(None, None, 'prow', None, 'pcol'), may hold values from -5 to 5
- child_v: bfloat16 [2, 10, 4, 2, 8, 512, 128], P(None, None, 'prow', None, 'pcol'), may hold values from -5 to 5
- child_rank: int32 [2, 10, 4, 2, 8], P(None, None, 'prow', None, 'pcol'), may hold values from 0 to 128, as said below
- diag_shift: float32 [16, 512], replicated, may hold values from 0.5 to 4
Outputs:
- front_out: float32 [10, 4, 512, 2, 8, 512], P(None, 'prow', None, None, 'pcol')
Inputs may be any that keep to these rules, and one draw needn't show every extreme that they name: `child_rank`: 0 on and above the block diagonal (i <= j); below it 0 where the child has no tile, else from 16 to 128.
All inputs are finite; a program needn't handle non-finite values.
Results may differ from a plain program's by a relative error of at most 0.0003.
Values may be sent and summed in bfloat16 or wider, within the bound.
A program may use at most 320 MiB of HBM per device.

v0:
```python
import functools

import jax
import jax.numpy as jnp
from jax import lax
from jax.experimental import pallas as pl
from jax.experimental.pallas import tpu as pltpu
from jax.sharding import PartitionSpec as P

PANELS = 2
STEP = 128
SUB = 8


def nt(a, b, precision=None):
    return lax.dot_general(
        a, b, (((1,), (1,)), ((), ())), preferred_element_type=jnp.float32, precision=precision
    )


def nn(a, b, precision=None):
    return lax.dot_general(
        a, b, (((1,), (0,)), ((), ())), preferred_element_type=jnp.float32, precision=precision
    )


def factor_kernel(s_ref, c_ref, y_ref, w_ref, e_ref):
    extent = s_ref.shape[0]
    exact = lax.Precision.HIGHEST
    w_ref[...] = s_ref[...]
    e_ref[...] = (
        lax.broadcasted_iota(jnp.int32, (extent, extent), 0)
        == lax.broadcasted_iota(jnp.int32, (extent, extent), 1)
    ).astype(jnp.float32)
    groups = STEP // SUB
    sub_row = lax.broadcasted_iota(jnp.int32, (SUB, STEP), 0)
    lane = lax.broadcasted_iota(jnp.int32, (SUB, STEP), 1)

    @pl.loop(0, extent // STEP)
    def _(block):
        base = pl.multiple_of(block * STEP, STEP)
        here = pl.ds(base, STEP)
        tile = w_ref[here, here]
        left = [tile[g * SUB : (g + 1) * SUB] for g in range(groups)]
        right = [(lane == sub_row + g * SUB).astype(jnp.float32) for g in range(groups)]
        for j in range(STEP):
            own, inner = divmod(j, SUB)
            row = left[own][inner : inner + 1]
            inverse = 1.0 / jnp.broadcast_to(row[:, j : j + 1], (1, STEP))
            row_left = jnp.broadcast_to(row * inverse, (SUB, STEP))
            row_right = jnp.broadcast_to(right[own][inner : inner + 1] * inverse, (SUB, STEP))
            for g in range(own, groups):
                weight = jnp.broadcast_to(left[g][:, j : j + 1], (SUB, STEP))
                if g == own:
                    weight = jnp.where(sub_row > inner, weight, 0.0)
                left[g] = left[g] - weight * row_left
                right[g] = right[g] - weight * row_right
        upper = jnp.concatenate(left, axis=0)
        lower_inverse = jnp.concatenate(right, axis=0)
        tile_row = lax.broadcasted_iota(jnp.int32, (STEP, STEP), 0)
        tile_col = lax.broadcasted_iota(jnp.int32, (STEP, STEP), 1)
        pivots = jnp.sum(jnp.where(tile_row == tile_col, upper, 0.0), axis=1, keepdims=True)
        root = jnp.sqrt(pivots)
        pivot_factor = (jnp.where(tile_row <= tile_col, upper, 0.0) / root).T
        pivot_inverse = lower_inverse / root
        panel = nt(w_ref[:, here], pivot_inverse, exact)
        below = lax.broadcasted_iota(jnp.int32, (extent, STEP), 0) >= base + STEP
        panel = jnp.where(below, panel, 0.0)
        c_ref[:, here] = panel
        c_ref[here, here] = pivot_factor
        solved = nn(pivot_inverse, e_ref[here, :], exact)
        y_ref[here, :] = solved
        w_ref[...] -= nt(panel, panel, exact)
        e_ref[...] -= nn(panel, solved, exact)


def factor(pivot_tile):
    shape = jax.ShapeDtypeStruct(pivot_tile.shape, jnp.float32)
    spec = pl.BlockSpec(memory_space=pltpu.VMEM)
    return pl.pallas_call(
        factor_kernel,
        out_shape=(shape, shape),
        in_specs=[spec],
        out_specs=(spec, spec),
        scratch_shapes=[pltpu.VMEM(pivot_tile.shape, jnp.float32)] * 2,
        compiler_params=pltpu.CompilerParams(vmem_limit_bytes=24 * 2**20),
        cost_estimate=pl.CostEstimate(
            flops=60_000_000_000, bytes_accessed=3 * 2**20, transcendentals=0
        ),
        name="factor",
    )(pivot_tile)


def finish_kernel(prow_count, pcol_count, at_ref, u_ref, v_ref, g_ref, h_ref, d_ref, p_ref, o_ref):
    t, r = pl.program_id(0), pl.program_id(1)
    i = r * prow_count + at_ref[0]
    j = t * pcol_count + at_ref[1]

    @pl.when(i < j)
    def _():
        o_ref[0] = jnp.zeros_like(o_ref[0])

    @pl.when((i >= j) & (j < PANELS))
    def _():
        o_ref[0] = p_ref[0]

    @pl.when((i >= j) & (j >= PANELS))
    def _():
        total = -nt(g_ref[0], h_ref[0])
        for c in range(u_ref.shape[0]):
            total += nt(u_ref[c, 0, 0], v_ref[c, 0, 0])
        o_ref[0] = total

    @pl.when((i == j) & (j >= PANELS))
    def _():
        o_ref[0] += d_ref[0]


def finish(prow_count, pcol_count, at, left, right, solved, other, diag, panels):
    children, rows, cols, extent, rank = left.shape
    wide = solved.shape[-1]
    factor_spec = pl.BlockSpec((children, 1, 1, extent, rank), lambda t, r, at: (0, r, t, 0, 0))
    return pl.pallas_call(
        functools.partial(finish_kernel, prow_count, pcol_count),
        out_shape=jax.ShapeDtypeStruct((rows, extent, cols * extent), jnp.float32),
        grid_spec=pltpu.PrefetchScalarGridSpec(
            num_scalar_prefetch=1,
            grid=(cols, rows),
            in_specs=[
                factor_spec,
                factor_spec,
                pl.BlockSpec((1, extent, wide), lambda t, r, at: (r, 0, 0)),
                pl.BlockSpec((1, extent, wide), lambda t, r, at: (t, 0, 0)),
                pl.BlockSpec((1, extent, extent), lambda t, r, at: (t, 0, 0)),
                pl.BlockSpec(
                    (1, extent, extent), lambda t, r, at: (jnp.where(t == 0, r, rows - 1), 0, 0)
                ),
            ],
            out_specs=pl.BlockSpec((1, extent, extent), lambda t, r, at: (r, 0, t)),
        ),
        compiler_params=pltpu.CompilerParams(vmem_limit_bytes=48 * 2**20),
        cost_estimate=pl.CostEstimate(
            flops=2 * rows * cols * extent * extent * (wide + children * rank),
            bytes_accessed=60 * 2**20,
            transcendentals=0,
        ),
        name="finish",
    )(at, left, right, solved, other, diag, panels)


def pieces(value, count):
    parts = []
    for _ in range(count):
        part = lax.reduce_precision(value, 8, 7)
        parts.append(part.astype(jnp.bfloat16))
        value = value - part
    return parts


def times(left_parts, right_parts, pattern):
    total = None
    for a in left_parts:
        for b in right_parts:
            term = jnp.einsum(pattern, a, b, preferred_element_type=jnp.float32)
            total = term if total is None else total + term
    return total


def on_device(child_u, child_v, child_rank, diag_shift):
    prow_count = lax.axis_size("prow")
    pcol_count = lax.axis_size("pcol")
    own_row = lax.axis_index("prow")
    own_column = lax.axis_index("pcol")
    both = ("prow", "pcol")
    rank_grid = child_rank[:, :, 0, :, 0]
    rows_here = rank_grid.shape[1]
    cols_here = rank_grid.shape[2]
    extent = child_u.shape[-2]
    keep_mask = (
        jnp.arange(child_u.shape[-1], dtype=jnp.int32)[None, None, None, :]
        < rank_grid[:, :, :, None]
    ).astype(jnp.bfloat16)
    left = child_u[:, :, 0, :, 0] * keep_mask[:, :, :, None, :]
    right = child_v[:, :, 0, :, 0] * keep_mask[:, :, :, None, :]
    kept_rows = cols_here * pcol_count // prow_count
    row_terms = jnp.einsum(
        "crtak,crtbk->rab", left[:, :kept_rows], left[:, :kept_rows],
        preferred_element_type=jnp.float32,
    )
    column_terms = [
        jnp.einsum(
            "crak,crbk->ab", right[:, :, t], right[:, :, t], preferred_element_type=jnp.float32
        )
        for t in range(cols_here)
    ]
    zero = jnp.zeros((extent, extent), jnp.float32)
    pivot_parts = []
    for k in range(PANELS):
        row, col = k // prow_count, k // pcol_count
        in_row = own_row == k % prow_count
        in_col = own_column == k % pcol_count
        part = jnp.where(in_col, column_terms[col], zero)
        part = part + jnp.where(in_row, row_terms[row], zero)
        own_tile = jnp.einsum(
            "cak,cbk->ab", left[:, row, col], right[:, row, col],
            preferred_element_type=jnp.float32,
        )
        pivot_parts.append(part + jnp.where(in_row & in_col, own_tile, zero))
    pivot_sums = lax.psum(jnp.stack(pivot_parts), both)

    pairs = [(m, k) for k in range(PANELS) for m in range(k + 1, PANELS)]
    pair_factors = []
    for m, k in pairs:
        root = (own_row == m % prow_count) & (own_column == k % pcol_count)
        tile = jnp.stack(
            [f[:, m // prow_count, k // pcol_count] for f in (left, right)]
        )
        pair_factors.append(jnp.where(root, tile, jnp.zeros_like(tile)))
    pair_factors = lax.psum(jnp.stack(pair_factors), both)

    panel_factors = []
    for k in range(PANELS):
        tiles = jnp.stack([f[:, :, k // pcol_count] for f in (left, right)])
        panel_factors.append(
            jnp.where(own_column == k % pcol_count, tiles, jnp.zeros_like(tiles))
        )
    panel_factors = lax.psum(jnp.stack(panel_factors), "pcol")

    block_rows = jnp.arange(rows_here, dtype=jnp.int32) * prow_count + own_row
    block_cols = jnp.arange(cols_here, dtype=jnp.int32) * pcol_count + own_column
    other_factors = jnp.take(panel_factors, block_cols // prow_count, axis=3)
    other_factors = lax.psum(
        jnp.where(own_row == own_column % prow_count, other_factors, jnp.zeros_like(other_factors)),
        "prow",
    )
    row_sums = lax.psum(row_terms, "pcol")
    column_sums = lax.psum(jnp.stack(column_terms), "prow")

    identity = jnp.eye(extent, dtype=jnp.float32)
    near_rows = jnp.concatenate([block_rows, block_cols])
    near_factors = jnp.concatenate([panel_factors, other_factors], axis=3)
    rounded = []
    fixed = {m: [] for m in range(PANELS)}
    panels = jnp.zeros((rows_here, extent, extent), jnp.float32)
    for k in range(PANELS):
        pivot_tile = pivot_sums[k] + identity * diag_shift[k][None, :]
        for g in fixed[k]:
            pivot_tile = pivot_tile - nt(g, g)
        lower, inverse = factor(pivot_tile)
        inverse_parts = pieces(inverse, 3)
        carried = [pieces(times(inverse_parts, [g], "ab,bk->ak"), 2) for g in fixed[k]]

        def solve(left_tiles, right_tiles, earlier):
            moved = times(inverse_parts, [right_tiles], "ab,crbk->crak")
            value = times([left_tiles], pieces(moved, 2), "crak,crbk->rab")
            for g, parts in zip(earlier, carried):
                value = value - times([g], parts, "rak,bk->rab")
            return value

        for position, (m, kk) in enumerate(pairs):
            if kk == k:
                tile = pair_factors[position]
                earlier = [g[None] for g in fixed[m]]
                value = solve(tile[0][:, None], tile[1][:, None], earlier)
                fixed[m].append(value[0].astype(jnp.bfloat16))
        value = solve(near_factors[k, 0], near_factors[k, 1], rounded)
        value = jnp.where((near_rows > k)[:, None, None], value, 0.0)
        rounded.append(value.astype(jnp.bfloat16))
        scale = jnp.diagonal(lower)
        panel = jnp.where(
            (block_rows == k)[:, None, None], lower[None], value[:rows_here]
        ) * scale[None, None, :]
        panels = jnp.where(own_column == k % pcol_count, panel, panels)

    wide = jnp.concatenate(rounded, axis=-1)
    select_cols = (
        block_cols[:, None] == jnp.arange(diag_shift.shape[0], dtype=jnp.int32)[None, :]
    ).astype(jnp.float32)
    shift_cols = jnp.dot(select_cols, diag_shift, precision=lax.Precision.HIGHEST)
    diag = (
        jnp.take(row_sums, block_cols // prow_count, axis=0)
        + column_sums
        + identity[None] * shift_cols[:, None, :]
    )
    at = jnp.stack([own_row, own_column]).astype(jnp.int32)
    out = finish(
        prow_count, pcol_count, at, left, right, wide[:rows_here], wide[rows_here:], diag, panels
    )
    return out.reshape(rows_here, 1, extent, cols_here, 1, extent)


def solution(mesh):
    placed = (
        P(None, None, "prow", None, "pcol", None, None),
        P(None, None, "prow", None, "pcol", None, None),
        P(None, None, "prow", None, "pcol"),
        P(),
    )
    return jax.shard_map(
        on_device,
        mesh=mesh,
        in_specs=placed,
        out_specs=P(None, "prow", None, None, "pcol", None),
        check_vma=False,
    )
```

profile of v0, /device:TPU:31, one launch (start us, length us, event | category | flops | bytes accessed | tf_op | source)
XLA Modules:
  0.0 1074.7 jit_solution(15455139120487339369)
XLA Ops:
  35.3 9.2 pad_maximum_fusion
  59.5 96.9 %all-reduce.11.cloned.1.call-done = f32[2,512,512]{2,1,0:T(8,128)} async-done(((f32[2,512,512]{2,1,0:T(8,128)}), f32[2,512,512]{2,1,0:T(8,128)}) %all-reduce.11.cloned.1.call-update) | async-done | bytes 2097168 | tf_op jit(solution)/shard_map/psum | solution.py:209
  157.8 52.7 %factor.2 = (f32[512,512]{1,0:T(8,128)S(1)}, f32[512,512]{1,0:T(8,128)S(1)}) custom-call(f32[512,512]{1,0:T(8,128)S(1)} %fusion.45.s_ref), custom_call_target="tpu_custom_call" | custom-call | flops 60000002048 | bytes 3145728 | tf_op jit(solution)/shard_map/factor/pallas_call | solution.py:80
  210.5 79.9 %all-reduce.13.cloned.1.call-done = bf16[1,2,2,512,128]{4,3,2,1,0:T(8,128)(2,1)} async-done(((bf16[1,2,2,512,128]{4,3,2,1,0:T(8,128)(2,1)}), bf16[1,2,2,512,128]{4,3,2,1,0:T(8,128)(2,1)}) %all-reduce.13.cloned.1.call-update) | async-done | bytes 524304 | tf_op jit(solution)/shard_map/psum | solution.py:219
  295.6 52.8 %factor.3 = (f32[512,512]{1,0:T(8,128)S(1)}, f32[512,512]{1,0:T(8,128)S(1)}) custom-call(f32[512,512]{1,0:T(8,128)S(1)} %convolution_subtract_fusion.s_ref), custom_call_target="tpu_custom_call" | custom-call | flops 60000002048 | bytes 3145728 | tf_op jit(solution)/shard_map/factor/pallas_call | solution.py:80
  351.3 269.7 %all-reduce.7.cloned.1.call-done = bf16[2,2,2,10,512,128]{5,4,2,3,1,0:T(8,128)(2,1)} async-done(((bf16[2,2,2,10,512,128]{5,4,2,3,1,0:T(8,128)(2,1)}), bf16[2,2,2,10,512,128]{5,4,2,3,1,0:T(8,128)(2,1)}) %all-reduce.7.cloned.1.call-update) | async-done | bytes 10485776 | tf_op jit(solution)/shard_map/psum | solution.py:227
  621.0 9.3 copy.40
  630.3 7.1 gather_fusion
  648.1 8.6 gather_fusion.2
  656.8 123.2 %all-reduce.15.cloned.1.call-done = f32[4,512,512]{2,1,0:T(8,128)} async-done(((f32[4,512,512]{2,1,0:T(8,128)}), f32[4,512,512]{2,1,0:T(8,128)}) %all-reduce.15.cloned.1.call-update) | async-done | bytes 4194320 | tf_op jit(solution)/shard_map/psum | solution.py:236
  784.2 49.6 %all-reduce.17.cloned.1.call-done = f32[2,512,512]{2,1,0:T(8,128)} async-done(((f32[2,512,512]{2,1,0:T(8,128)}), f32[2,512,512]{2,1,0:T(8,128)}) %all-reduce.17.cloned.1.call-update) | async-done | bytes 2097168 | tf_op jit(solution)/shard_map/psum | solution.py:237
  838.2 11.4 %constant_dynamic-update-slice_fusion.1 = bf16[2,2,2,12,512,128]{5,4,2,3,1,0:T(8,128)(2,1)} fusion(bf16[2,2,2,10,512,128]{5,4,2,3,1,0:T(8,128)(2,1)} %all-reduce.7.cloned.1.call-done), kind=kLoop, calls=%fused_computation.145 | loop fusion | bytes 20971520
  849.7 37.8 %all-reduce.9.cloned.1.call-done = bf16[2,2,2,2,512,128]{5,4,2,3,1,0:T(8,128)(2,1)} async-done(((bf16[2,2,2,2,512,128]{5,4,2,3,1,0:T(8,128)(2,1)}), bf16[2,2,2,2,512,128]{5,4,2,3,1,0:T(8,128)(2,1)}) %all-reduce.9.cloned.1.call-update) | async-done | bytes 2097168 | tf_op jit(solution)/shard_map/psum | solution.py:232
  911.9 7.5 fusion.16
  919.4 12.8 %fusion.91 = (bf16[12,512,512]{2,1,0:T(8,128)(2,1)S(1)}, f32[12,512,512]{2,1,0:T(8,128)}) fusion(bf16[2,12,512,128]{2,3,1,0:T(8,128)(2,1)} %get-tuple-element.17, bf16[2,2,2,12,512,128]{5,4,2,3,1,0:T(8,128)(2,1)} %constant_dynamic-update-slice_fusion, f32[12,512,512,1]{2,1,3,0:T(8,128)} %fusion.16, pred[12]{0:T(512)(128)(4,1)S(1)} %copy-done.15), kind=kOutput, calls=%fused_computation.177 | convolution fusion | flops 1620049920 | bytes 37748748 | tf_op jit(solution)/shard_map/crak,crbk->rab/dot_general | solution.py:164
  932.2 6.7 fusion.55
  939.6 6.5 fusion.58
  946.1 5.5 fusion.11
  951.7 7.6 fusion.13
  959.3 21.3 %fusion.92 = (bf16[12,512,512]{2,1,0:T(8,128)(2,1)}, f32[12,512,512]{2,1,0:T(8,128)}) fusion(f32[12,512,512]{2,1,0:T(8,128)} %fusion.58, f32[12,512,512]{2,1,0:T(8,128)} %fusion.55, bf16[2,12,512,128]{2,3,1,0:T(8,128)(2,1)S(1)} %get-tuple-element.15, bf16[2,2,2,12,512,128]{5,4,2,3,1,0:T(8,128)(2,1)} %constant_dynamic-update-slice_fusion, ...), kind=kOutput, calls=%fused_computation.178 | convolution fusion | flops 1626341376 | bytes 62914572 | tf_op jit(solution)/shard_map/crak,crbk->rab/dot_general | solution.py:164
  984.0 9.9 fusion.3.g_ref
  993.9 10.5 fusion.6.p_ref
  1004.4 32.3 %finish.1 = f32[10,512,1024]{2,1,0:T(8,128)} custom-call(s32[2]{0:T(128)S(1)} %pad_add_fusion.at_ref, bf16[2,10,2,512,128]{4,3,2,1,0:T(8,128)(2,1)} %copy.67.u_ref, bf16[2,10,2,512,128]{4,3,2,1,0:T(8,128)(2,1)} %copy-done.7, bf16[10,512,1024]{2,1,0:T(8,128)(2,1)} %fusion.3.g_ref, bf16[2,512,1024]{2,1,0:T(8,128)(2,1)S(1)} %pad_maximum_fusion.2.h_ref, ...), custom_call_target="tpu_custom_call" | custom-call | flops 13421772800 | bytes 62914560 | tf_op jit(solution)/shard_map/finish/pallas_call | solution.py:123
  1036.7 30.9 %reshape.327 = f32[10,1,512,2,1,512]{5,4,3,2,1,0:T(1,128)} reshape(f32[10,512,1024]{2,1,0:T(8,128)} %finish.1) | data formatting | bytes 41943040 | tf_op jit(solution)/shard_map/reshape | solution.py:289
  (117 shorter events, 100.9 us)
Async XLA Ops:
  6.5 149.9 %all-reduce.11.cloned.1.call-start = ((), (), s32[]{:S(2)}) async-start(), calls=%async_computation.2 | async-start | bytes 4194304 | tf_op jit(solution)/shard_map/psum | solution.py:209
  10.3 4.7 copy-start.7
  23.9 266.5 %all-reduce.13.cloned.1.call-start = ((), (), s32[]{:S(2)}) async-start(), calls=%async_computation.3 | async-start | bytes 1048576 | tf_op jit(solution)/shard_map/psum | solution.py:219
  26.8 594.2 %all-reduce.7.cloned.1.call-start = ((), (), s32[]{:S(2)}) async-start(), calls=%async_computation | async-start | bytes 20971520 | tf_op jit(solution)/shard_map/psum | solution.py:227
  44.5 735.5 %all-reduce.15.cloned.1.call-start = ((), (), s32[]{:S(2)}) async-start(), calls=%async_computation.4 | async-start | bytes 8388608 | tf_op jit(solution)/shard_map/psum | solution.py:236
  45.1 788.7 %all-reduce.17.cloned.1.call-start = ((), (), s32[]{:S(2)}) async-start(), calls=%async_computation.5 | async-start | bytes 4194304 | tf_op jit(solution)/shard_map/psum | solution.py:237
  50.8 836.7 %all-reduce.9.cloned.1.call-start = ((), (), s32[]{:S(2)}) async-start(), calls=%async_computation.1 | async-start | bytes 4194304 | tf_op jit(solution)/shard_map/psum | solution.py:232
  53.1 5.5 copy-start.18
  290.4 4.8 copy-start.13
  295.2 54.7 %copy-start.9 = (bf16[512,512]{1,0:T(8,128)(2,1)}, bf16[512,512]{1,0:T(8,128)(2,1)S(1)}, u32[]{:S(2)}) copy-start(bf16[512,512]{1,0:T(8,128)(2,1)S(1)} %fusion.36) | copy-start | bytes 1572868
  911.9 7.5 copy-start.15
  919.4 12.8 %copy-start.10 = (f32[512,512]{1,0:T(8,128)S(1)}, f32[512,512]{1,0:T(8,128)}, u32[]{:S(2)}) copy-start(f32[512,512]{1,0:T(8,128)} %convolution_add_fusion) | copy-start | bytes 3145732
  932.2 7.4 copy-start.3
  932.2 13.9 %slice-start.3 = ((s8[6291456]{0:T(1024)(128)(4,1)}), s8[4194304]{0:T(1024)(128)(4,1)S(1)}, s32[]{:S(2)}) async-start(s8[6291456]{0:T(1024)(128)(4,1)} %bitcast.218), calls=%async_computation.9 | async-start | bytes 8388608
  939.6 6.6 copy-start.6
  939.6 6.6 slice-start.4
  951.7 7.6 copy-start.14
  980.6 13.3 %slice-start = ((s8[12582912]{0:T(1024)(128)(4,1)}), s8[4194304]{0:T(1024)(128)(4,1)S(1)}, s32[]{:S(2)}) async-start(s8[12582912]{0:T(1024)(128)(4,1)} %bitcast.216), calls=%async_computation.6 | async-start | bytes 8388608
  980.6 13.3 %slice-start.1 = ((s8[12582912]{0:T(1024)(128)(4,1)}), s8[4194304]{0:T(1024)(128)(4,1)S(1)}, s32[]{:S(2)}) async-start(s8[12582912]{0:T(1024)(128)(4,1)} %bitcast.216), calls=%async_computation.7 | async-start | bytes 8388608
  984.0 9.9 copy-start.1
  984.0 9.9 slice-start.2
  984.0 9.9 copy-start.16
  984.0 9.9 copy-start.17
  993.9 10.5 copy-start.2
  (6 other events, 19.8 us)
Sparse Core Ops, SparseCore 0:
  24.0 132.3 all-reduce.10
  161.7 128.6 all-reduce.12
  294.3 326.6 all-reduce.6
  624.5 155.3 all-reduce.14
  782.2 51.4 all-reduce.16
  835.9 51.4 all-reduce.8
where the time goes:
time: 1080 us; the launch traced here: 1070 us
  waiting for transfers between devices  658 us (61%)
  Pallas kernels  138 us (13%)
  matrix products  106 us (10%)
  local copies, waits for them, and re-layouts  103 us (10%)
  other arithmetic  54.6 us (5%)
  between operations  14.1 us (1%)
    psum x1, waiting for transfers between devices, on_device(): panel_factors = lax.psum(jnp.stack(panel_factors), 'pcol')  270 us
    psum x1, waiting for transfers between devices, on_device(): row_sums = lax.psum(row_terms, 'pcol')  123 us
    pallas_call x2, Pallas kernels, factor(): pl.pallas_call(factor_kernel, out_shape=(shape, shape), in_specs=[spec],...  106 us
    psum x1, waiting for transfers between devices, on_device(): pivot_sums = lax.psum(jnp.stack(pivot_parts), both)  96.9 us
    dot_general x20, matrix products, times(): term = jnp.einsum(pattern, a, b, preferred_element_type=jnp.float32)  95.1 us
    psum x1, waiting for transfers between devices, on_device(): pair_factors = lax.psum(jnp.stack(pair_factors), both)  79.9 us
    psum x1, waiting for transfers between devices, on_device(): column_sums = lax.psum(jnp.stack(column_terms), 'prow')  49.6 us
    psum x1, waiting for transfers between devices, on_device(): lax.psum(jnp.where(own_row == own_column % prow_count, other_factors, jnp...  37.8 us
  transfers between devices with their start and end apart: 6, of which 6 were waited for; matrix products, arithmetic and copies ran while one was open for 9% of the time, Pallas kernels for 10%

commit v1 on v0

v1 whole, which is shorter than its diff:
```python
import functools

import jax
import jax.numpy as jnp
from jax import lax
from jax.experimental import pallas as pl
from jax.experimental.pallas import tpu as pltpu
from jax.sharding import PartitionSpec as P

PANELS = 2
STEP = 128
SUB = 8
PAIRS = [(m, k) for k in range(PANELS) for m in range(k + 1, PANELS)]
MESH = pl.DeviceIdType.MESH
ANY = pl.BlockSpec(memory_space=pl.ANY)


def nt(a, b, precision=None):
    return lax.dot_general(
        a, b, (((1,), (1,)), ((), ())), preferred_element_type=jnp.float32, precision=precision
    )


def nn(a, b, precision=None):
    return lax.dot_general(
        a, b, (((1,), (0,)), ((), ())), preferred_element_type=jnp.float32, precision=precision
    )


def split(value):
    high = value.astype(jnp.bfloat16)
    low = (value - high.astype(jnp.float32)).astype(jnp.bfloat16)
    return high, low


def prep_kernel(dims, at_ref, rank_ref, u_ref, v_ref, pan_ref, sum_ref, row_ref):
    prow, pcol, kept, tiles = dims
    r = pl.program_id(0)
    children, cols = u_ref.shape[0], u_ref.shape[3]
    rank_max = u_ref.shape[-1]
    lane = lax.broadcasted_iota(jnp.int32, (1, rank_max), 1)

    @pl.when(r == 0)
    def _():
        sum_ref[...] = jnp.zeros_like(sum_ref)

    for t in range(cols):
        left, right = [], []
        for c in range(children):
            rank = rank_ref[(c * pl.num_programs(0) + r) * cols + t]
            keep = (lane < rank).astype(jnp.bfloat16)
            left.append(u_ref[c, 0, 0, t, 0] * keep)
            right.append(v_ref[c, 0, 0, t, 0] * keep)
        if t == 0:
            for c in range(children):
                pan_ref[0, 0, 0, c] = left[c]
                pan_ref[0, 0, 1, c] = right[c]
        if t < tiles:

            @pl.when(r < kept)
            def _(left=left, t=t):
                for c in range(children):
                    row_ref[0, t, c] = left[c]

        wide = jnp.concatenate(right, axis=1)
        sum_ref[t] += nt(wide, wide)
        i = r * prow + at_ref[0]
        j = t * pcol + at_ref[1]

        @pl.when((i == j) & (j < PANELS))
        def _(left=left, wide=wide, t=t):
            sum_ref[t] += nt(jnp.concatenate(left, axis=1), wide)


def prep(prow, pcol, kept, tiles, at, ranks, child_u, child_v):
    children, rows, _, cols, _, extent, rank = child_u.shape
    tile = pl.BlockSpec(
        (children, 1, 1, cols, 1, extent, rank), lambda r, at, ranks: (0, r, 0, 0, 0, 0, 0)
    )
    return pl.pallas_call(
        functools.partial(prep_kernel, (prow, pcol, kept, tiles)),
        out_shape=(
            jax.ShapeDtypeStruct((PANELS, rows, 2, children, extent, rank), jnp.bfloat16),
            jax.ShapeDtypeStruct((cols, extent, extent), jnp.float32),
            jax.ShapeDtypeStruct((kept, tiles, children, extent, rank), jnp.bfloat16),
        ),
        grid_spec=pltpu.PrefetchScalarGridSpec(
            num_scalar_prefetch=2,
            grid=(rows,),
            in_specs=[tile, tile],
            out_specs=(
                pl.BlockSpec(
                    (1, 1, 2, children, extent, rank),
                    lambda r, at, ranks: (lax.rem(at[1], PANELS), r, 0, 0, 0, 0),
                ),
                pl.BlockSpec((cols, extent, extent), lambda r, at, ranks: (0, 0, 0)),
                pl.BlockSpec(
                    (1, tiles, children, extent, rank),
                    lambda r, at, ranks: (jnp.minimum(r, kept - 1), 0, 0, 0, 0),
                ),
            ),
        ),
        compiler_params=pltpu.CompilerParams(vmem_limit_bytes=40 * 2**20),
        cost_estimate=pl.CostEstimate(
            flops=2 * rows * cols * extent * extent * children * rank,
            bytes_accessed=18 * 2**20,
            transcendentals=0,
        ),
        name="prep",
    )(at, ranks, child_u, child_v)


def exchange_kernel(dims, pan_in, sum_ref, row_ref, pan, oth, rowbuf, sumbuf, piv, pair, *scratch):
    prow, pcol, rows, cols, kept, tiles = dims
    (part, total, bounce, local, part_s, part_r, sum_s, sum_r, row_s, row_r, chain_s, chain_r,
     cross_s, cross_r, oth_s, oth_r, pair_s, pair_r, gat_s, gat_r) = scratch
    del pan_in
    p, q = lax.axis_index("prow"), lax.axis_index("pcol")
    z, y = q // PANELS, lax.rem(q, PANELS)
    depth = pcol // PANELS
    home = lax.rem(q, prow)
    extent = sum_ref.shape[-1]
    band = extent // prow

    barrier = pltpu.get_barrier_semaphore()
    for d in range(1, pcol):
        pl.semaphore_signal(
            barrier, inc=1, device_id={"pcol": lax.rem(q + d, pcol)}, device_id_type=MESH
        )
    for d in range(1, prow):
        pl.semaphore_signal(
            barrier, inc=1, device_id={"prow": lax.rem(p + d, prow)}, device_id_type=MESH
        )
    pl.semaphore_wait(barrier, pcol + prow - 2)

    def send(src, dst, send_sem, recv_sem, **target):
        return pltpu.make_async_remote_copy(
            src_ref=src, dst_ref=dst, send_sem=send_sem, recv_sem=recv_sem,
            device_id=target, device_id_type=MESH,
        )

    def part_copy(d):
        s = lax.rem(p + d, prow)
        return send(
            sum_ref.at[0, pl.ds(pl.multiple_of(s * band, 8), band)], part.at[d],
            part_s.at[d - 1], part_r.at[d - 1], prow=s,
        )

    def sum_copy():
        d = lax.rem(home + prow - p, prow) - 1
        return send(sum_ref, sumbuf.at[d], sum_s, sum_r.at[d], prow=home)

    def sum_arrival(d):
        return send(sum_ref, sumbuf.at[d], sum_s, sum_r.at[d], prow=home)

    def reach(r):
        return sum(1 for t in range(tiles) if t * pcol < (r + 1) * prow)

    def row_copy(r, first):
        i = r * prow + p
        owner, slot = lax.rem(i, pcol), i // pcol
        window = pl.ds(first, reach(r) - first)
        return send(
            row_ref.at[r, window], rowbuf.at[slot, q, window], row_s.at[r], row_r.at[slot, q],
            pcol=owner,
        )

    def row_arrival(slot, origin, r, first):
        window = pl.ds(first, reach(r) - first)
        return send(
            row_ref.at[r, window], rowbuf.at[slot, origin, window], row_s.at[r],
            row_r.at[slot, origin], pcol=origin,
        )

    def chain_copy(n):
        ref = pan.at[y, n // 2, n % 2] if n < 2 * rows else piv.at[y, p]
        return send(ref, ref, chain_s.at[n], chain_r.at[n], pcol=q + PANELS)

    def cross_copy(n, which):
        ref = pan.at[which, n // 2, n % 2] if n < 2 * rows else piv.at[which, p]
        return send(ref, ref, cross_s.at[n], cross_r.at[n], pcol=q + 1 - 2 * y)

    def forward(n):
        @pl.when(z < depth - 1)
        def _():
            chain_copy(n).start()

        cross_copy(n, y).start()

    def oth_row(t):
        return (t * pcol + q) // prow

    def oth_copy(t, k, d):
        n = t * PANELS + k
        return send(
            pan.at[k, oth_row(t)], oth.at[t, k], oth_s.at[n, d - 1], oth_r.at[n],
            prow=lax.rem(p + d, prow),
        )

    def pair_copy(n, d):
        m, k = PAIRS[n]
        return send(
            pan.at[k, m // prow], pair.at[n], pair_s.at[n, d - 1], pair_r.at[n],
            prow=lax.rem(p + d, prow),
        )

    def gat_copy(k, d):
        return send(
            piv.at[k, p], piv.at[k, p], gat_s.at[k, d - 1], gat_r.at[k, d - 1],
            prow=lax.rem(p + d, prow),
        )

    def gat_arrival(k, d):
        o = lax.rem(p + prow - d, prow)
        return send(
            piv.at[k, o], piv.at[k, o], gat_s.at[k, d - 1], gat_r.at[k, d - 1], prow=o
        )

    @pl.when(z == 0)
    def _():
        for d in range(1, prow):
            part_copy(d).start()
        pltpu.make_async_copy(
            sum_ref.at[0, pl.ds(pl.multiple_of(p * band, 8), band)], part.at[0], local.at[0]
        ).start()

    @pl.when(p != home)
    def _():
        sum_copy().start()

    for r in range(kept):
        owner = lax.rem(r * prow + p, pcol)

        @pl.when((q != owner) & (z > 0))
        def _():
            row_copy(r, 0).start()

        if reach(r) > 1:

            @pl.when((q != owner) & (z == 0))
            def _():
                row_copy(r, 1).start()

    last = 2 * rows

    def step(n):
        @pl.when(z > 0)
        def _():
            chain_copy(n).wait_recv()

        forward(n)

    step(0)
    step(1)

    @pl.when(z == 0)
    def _():
        pltpu.make_async_copy(
            sum_ref.at[0, pl.ds(pl.multiple_of(p * band, 8), band)], part.at[0], local.at[0]
        ).wait()
        for d in range(1, prow):
            part_copy(d).wait_recv()
        value = part[0]
        for d in range(1, prow):
            value = value + part[d]
        total[...] = value
        out = pltpu.make_async_copy(total, piv.at[y, p], local.at[1])
        out.start()
        out.wait()

    step(last)
    near = 2 * kept
    for n in range(2, near + 2):
        step(n)

    cross_copy(last, 1 - y).wait_recv()
    for n in range(near):
        cross_copy(n, 1 - y).wait_recv()

    for k in range(PANELS):
        for d in range(1, prow):
            gat_copy(k, d).start()
    for n, (m, k) in enumerate(PAIRS):

        @pl.when(p == m % prow)
        def _():
            for d in range(1, prow):
                pair_copy(n, d).start()
            slot = cols * PANELS + n
            load = pltpu.make_async_copy(pan.at[k, m // prow], bounce.at[slot], local.at[2 + slot])
            load.start()
            load.wait()
            store = pltpu.make_async_copy(bounce.at[slot], pair.at[n], local.at[2 + slot])
            store.start()
            store.wait()

    @pl.when(p == home)
    def _():
        for t in range(cols):
            for k in range(PANELS):
                for d in range(1, prow):
                    oth_copy(t, k, d).start()
        loads = [
            pltpu.make_async_copy(
                pan.at[k, oth_row(t)], bounce.at[t * PANELS + k], local.at[2 + t * PANELS + k]
            )
            for t in range(cols)
            for k in range(PANELS)
        ]
        stores = [
            pltpu.make_async_copy(
                bounce.at[t * PANELS + k], oth.at[t, k], local.at[2 + t * PANELS + k]
            )
            for t in range(cols)
            for k in range(PANELS)
        ]
        for load in loads:
            load.start()
        for load, store in zip(loads, stores):
            load.wait()
            store.start()
        for store in stores:
            store.wait()

    for n in range(near + 2, last):
        step(n)
    for n in range(near, last):
        cross_copy(n, 1 - y).wait_recv()

    for k in range(PANELS):
        for d in range(1, prow):
            gat_arrival(k, d).wait_recv()
            gat_copy(k, d).wait_send()
    for n, (m, k) in enumerate(PAIRS):

        @pl.when(p == m % prow)
        def _():
            for d in range(1, prow):
                pair_copy(n, d).wait_send()

        @pl.when(p != m % prow)
        def _():
            pair_copy(n, 1).wait_recv()

    @pl.when(p == home)
    def _():
        for t in range(cols):
            for k in range(PANELS):
                for d in range(1, prow):
                    oth_copy(t, k, d).wait_send()
        for d in range(prow - 1):
            sum_arrival(d).wait_recv()
        for slot in range(cols):
            for origin in range(pcol):

                @pl.when(q != origin)
                def _():
                    low = slot * pcol // prow
                    first = 1 if origin < PANELS else 0
                    if reach(low) > first:
                        row_arrival(slot, origin, low, first).wait_recv()

    @pl.when(p != home)
    def _():
        for t in range(cols):
            for k in range(PANELS):
                oth_copy(t, k, 1).wait_recv()
        sum_copy().wait_send()

    @pl.when(z == 0)
    def _():
        for d in range(1, prow):
            part_copy(d).wait_send()

    for r in range(kept):
        owner = lax.rem(r * prow + p, pcol)

        @pl.when((q != owner) & (z > 0))
        def _():
            row_copy(r, 0).wait_send()

        if reach(r) > 1:

            @pl.when((q != owner) & (z == 0))
            def _():
                row_copy(r, 1).wait_send()

    for n in range(last + 1):

        @pl.when(z < depth - 1)
        def _():
            chain_copy(n).wait_send()

        cross_copy(n, y).wait_send()


def exchange(prow, pcol, pan, sums, rowtiles):
    _, rows, _, children, extent, rank = pan.shape
    cols = sums.shape[0]
    kept, tiles = rowtiles.shape[:2]
    band = extent // prow
    pairs = max(len(PAIRS), 1)
    dma = pltpu.SemaphoreType.DMA
    return pl.pallas_call(
        functools.partial(exchange_kernel, (prow, pcol, rows, cols, kept, tiles)),
        out_shape=(
            jax.ShapeDtypeStruct(pan.shape, pan.dtype),
            jax.ShapeDtypeStruct((cols, PANELS, 2, children, extent, rank), pan.dtype),
            jax.ShapeDtypeStruct((cols, pcol, tiles, children, extent, rank), pan.dtype),
            jax.ShapeDtypeStruct((prow - 1, cols, extent, extent), jnp.float32),
            jax.ShapeDtypeStruct((PANELS, prow, band, extent), jnp.float32),
            jax.ShapeDtypeStruct((pairs, 2, children, extent, rank), pan.dtype),
        ),
        in_specs=[ANY, ANY, ANY],
        out_specs=(ANY,) * 6,
        scratch_shapes=[
            pltpu.VMEM((prow, band, extent), jnp.float32),
            pltpu.VMEM((band, extent), jnp.float32),
            pltpu.VMEM((cols * PANELS + pairs, 2, children, extent, rank), pan.dtype),
            dma((2 + cols * PANELS + pairs,)),
            dma((prow - 1,)),
            dma((prow - 1,)),
            dma,
            dma((prow - 1,)),
            dma((kept,)),
            dma((cols, pcol)),
            dma((2 * rows + 1,)),
            dma((2 * rows + 1,)),
            dma((2 * rows + 1,)),
            dma((2 * rows + 1,)),
            dma((cols * PANELS, prow - 1)),
            dma((cols * PANELS,)),
            dma((pairs, prow - 1)),
            dma((pairs,)),
            dma((PANELS, prow - 1)),
            dma((PANELS, prow - 1)),
        ],
        input_output_aliases={0: 0},
        compiler_params=pltpu.CompilerParams(
            collective_id=0, has_side_effects=True, vmem_limit_bytes=40 * 2**20
        ),
        cost_estimate=pl.CostEstimate(
            flops=120_000_000_000, bytes_accessed=60 * 2**20, transcendentals=0
        ),
        name="exchange",
    )(pan, sums, rowtiles)


def factor_step(w_ref, e_ref, c_ref, y_ref):
    extent = w_ref.shape[0]
    exact = lax.Precision.HIGHEST
    groups = STEP // SUB
    sub_row = lax.broadcasted_iota(jnp.int32, (SUB, STEP), 0)
    lane = lax.broadcasted_iota(jnp.int32, (SUB, STEP), 1)

    @pl.loop(0, extent // STEP)
    def _(block):
        base = pl.multiple_of(block * STEP, STEP)
        here = pl.ds(base, STEP)
        tile = w_ref[here, here]
        left = [tile[g * SUB : (g + 1) * SUB] for g in range(groups)]
        right = [(lane == sub_row + g * SUB).astype(jnp.float32) for g in range(groups)]
        for j in range(STEP):
            own, inner = divmod(j, SUB)
            row = left[own][inner : inner + 1]
            inverse = 1.0 / jnp.broadcast_to(row[:, j : j + 1], (1, STEP))
            row_left = jnp.broadcast_to(row * inverse, (SUB, STEP))
            row_right = jnp.broadcast_to(right[own][inner : inner + 1] * inverse, (SUB, STEP))
            for g in range(own, groups):
                weight = jnp.broadcast_to(left[g][:, j : j + 1], (SUB, STEP))
                if g == own:
                    weight = jnp.where(sub_row > inner, weight, 0.0)
                left[g] = left[g] - weight * row_left
                right[g] = right[g] - weight * row_right
        upper = jnp.concatenate(left, axis=0)
        lower_inverse = jnp.concatenate(right, axis=0)
        tile_row = lax.broadcasted_iota(jnp.int32, (STEP, STEP), 0)
        tile_col = lax.broadcasted_iota(jnp.int32, (STEP, STEP), 1)
        pivots = jnp.sum(jnp.where(tile_row == tile_col, upper, 0.0), axis=1, keepdims=True)
        root = jnp.sqrt(pivots)
        pivot_factor = (jnp.where(tile_row <= tile_col, upper, 0.0) / root).T
        pivot_inverse = lower_inverse / root
        panel = nt(w_ref[:, here], pivot_inverse, exact)
        below = lax.broadcasted_iota(jnp.int32, (extent, STEP), 0) >= base + STEP
        panel = jnp.where(below, panel, 0.0)
        c_ref[:, here] = panel
        c_ref[here, here] = pivot_factor
        solved = nn(pivot_inverse, e_ref[here, :], exact)
        y_ref[here, :] = solved
        w_ref[...] -= nt(panel, panel, exact)
        e_ref[...] -= nn(panel, solved, exact)


def pivot_kernel(piv_ref, shift_ref, pair_ref, c_ref, inv_ref, car_ref, w_ref, e_ref, y_ref, g_ref):
    extent = w_ref.shape[0]
    children = pair_ref.shape[2]
    eye = lax.broadcasted_iota(jnp.int32, (extent, extent), 0) == lax.broadcasted_iota(
        jnp.int32, (extent, extent), 1
    )

    def wide(n, side):
        return jnp.concatenate([pair_ref[n, side, c] for c in range(children)], axis=1)

    @pl.loop(0, PANELS)
    def _(k):
        w_ref[...] = piv_ref[k] + jnp.where(eye, shift_ref[k], 0.0)
        for n, (m, _) in enumerate(PAIRS):

            @pl.when(k == m)
            def _():
                left = wide(n, 0)
                g = g_ref[n]
                w_ref[...] += nt(left, left) - nt(g, g)

        e_ref[...] = eye.astype(jnp.float32)
        factor_step(w_ref, e_ref, c_ref.at[k], y_ref)
        high, low = split(y_ref[...])
        inv_ref[k, 0] = high
        inv_ref[k, 1] = low

        for n, (m, kk) in enumerate(PAIRS):

            @pl.when(k == kk)
            def _():
                right = wide(n, 1)
                moved = split(nn(high, right) + nn(low, right))
                left = wide(n, 0)
                value = nt(left, moved[0]) + nt(left, moved[1])
                for o, (mo, ko) in enumerate(PAIRS):
                    if mo == m and ko < kk:
                        carry = [car_ref[PAIRS.index((kk, ko)), s] for s in range(2)]
                        value = value - nt(g_ref[o], carry[0]) - nt(g_ref[o], carry[1])
                g_ref[n] = value.astype(jnp.bfloat16)

            @pl.when(k == m)
            def _():
                g = g_ref[n]
                one, two = split(nn(high, g) + nn(low, g))
                car_ref[n, 0] = one
                car_ref[n, 1] = two


def pivots(piv, shift, pair):
    extent = piv.shape[-1]
    pairs = pair.shape[0]
    spec = pl.BlockSpec(memory_space=pltpu.VMEM)
    square = (extent, extent)
    return pl.pallas_call(
        pivot_kernel,
        out_shape=(
            jax.ShapeDtypeStruct((PANELS,) + square, jnp.float32),
            jax.ShapeDtypeStruct((PANELS, 2) + square, jnp.bfloat16),
            jax.ShapeDtypeStruct((pairs, 2) + square, jnp.bfloat16),
        ),
        in_specs=[spec] * 3,
        out_specs=(spec,) * 3,
        scratch_shapes=[
            pltpu.VMEM(square, jnp.float32),
            pltpu.VMEM(square, jnp.float32),
            pltpu.VMEM(square, jnp.float32),
            pltpu.VMEM((pairs,) + square, jnp.bfloat16),
        ],
        compiler_params=pltpu.CompilerParams(vmem_limit_bytes=40 * 2**20),
        cost_estimate=pl.CostEstimate(
            flops=100_000_000_000, bytes_accessed=8 * 2**20, transcendentals=0
        ),
        name="pivots",
    )(piv, shift, pair)


def solve_kernel(dims, at_ref, pan_ref, oth_ref, inv_ref, car_ref, c_ref, g_ref, p_ref):
    prow, pcol, rows = dims
    n = pl.program_id(0)
    children = pan_ref.shape[3]
    extent = inv_ref.shape[-1]
    row = n * prow + at_ref[0]
    col = (n - rows) * pcol + at_ref[1]
    index = jnp.where(n < rows, row, col)

    def body(source):
        solved = []
        for k in range(PANELS):
            left = jnp.concatenate([source(k, 0, c) for c in range(children)], axis=1)
            right = jnp.concatenate([source(k, 1, c) for c in range(children)], axis=1)
            moved = split(nn(inv_ref[k, 0], right) + nn(inv_ref[k, 1], right))
            value = nt(left, moved[0]) + nt(left, moved[1])
            for kk in range(k):
                slot = PAIRS.index((k, kk))
                value = value - nt(solved[kk], car_ref[slot, 0]) - nt(solved[kk], car_ref[slot, 1])
            value = jnp.where(index > k, value, 0.0)
            solved.append(value.astype(jnp.bfloat16))
            g_ref[0, :, k * extent : (k + 1) * extent] = solved[k]

            @pl.when((at_ref[1] == k) & (n < rows))
            def _(value=value, k=k):
                lower = c_ref[k]
                diagonal = lax.broadcasted_iota(
                    jnp.int32, lower.shape, 0
                ) == lax.broadcasted_iota(jnp.int32, lower.shape, 1)
                scale = jnp.sum(jnp.where(diagonal, lower, 0.0), axis=0, keepdims=True)
                p_ref[0] = jnp.where(index == k, lower, value) * scale

    @pl.when(n < rows)
    def _():
        body(lambda k, side, c: pan_ref[k, 0, side, c])

    @pl.when(n >= rows)
    def _():
        body(lambda k, side, c: oth_ref[0, k, side, c])


def solve(prow, pcol, at, pan, oth, inv, car, lower):
    _, rows, _, children, extent, rank = pan.shape
    cols = oth.shape[0]

    def whole(array):
        return pl.BlockSpec(array.shape, lambda n, at: (0,) * array.ndim)

    return pl.pallas_call(
        functools.partial(solve_kernel, (prow, pcol, rows)),
        out_shape=(
            jax.ShapeDtypeStruct((rows + cols, extent, PANELS * extent), jnp.bfloat16),
            jax.ShapeDtypeStruct((rows, extent, extent), jnp.float32),
        ),
        grid_spec=pltpu.PrefetchScalarGridSpec(
            num_scalar_prefetch=1,
            grid=(rows + cols,),
            in_specs=[
                pl.BlockSpec(
                    (PANELS, 1, 2, children, extent, rank),
                    lambda n, at: (0, jnp.minimum(n, rows - 1), 0, 0, 0, 0),
                ),
                pl.BlockSpec(
                    (1, PANELS, 2, children, extent, rank),
                    lambda n, at: (jnp.maximum(n - rows, 0), 0, 0, 0, 0, 0),
                ),
                whole(inv),
                whole(car),
                whole(lower),
            ],
            out_specs=(
                pl.BlockSpec((1, extent, PANELS * extent), lambda n, at: (n, 0, 0)),
                pl.BlockSpec(
                    (1, extent, extent),
                    lambda n, at: (jnp.where(at[1] < PANELS, jnp.minimum(n, rows - 1), 0), 0, 0),
                ),
            ),
        ),
        compiler_params=pltpu.CompilerParams(vmem_limit_bytes=56 * 2**20),
        cost_estimate=pl.CostEstimate(
            flops=22_000_000_000, bytes_accessed=40 * 2**20, transcendentals=0
        ),
        name="solve",
    )(at, pan, oth, inv, car, lower)


def diag_kernel(dims, at_ref, rowbuf, pan_ref, own_ref, sums_ref, mine_ref, shift_ref, d_ref):
    prow, pcol, kept = dims
    slot = pl.program_id(0)
    tiles, children, extent = rowbuf.shape[2], rowbuf.shape[3], rowbuf.shape[4]
    q = at_ref[1]

    @pl.when(at_ref[0] == lax.rem(q, prow))
    def _():
        eye = lax.broadcasted_iota(jnp.int32, (extent, extent), 0) == lax.broadcasted_iota(
            jnp.int32, (extent, extent), 1
        )
        total = mine_ref[0] + jnp.where(eye, shift_ref[0], 0.0)
        for s in range(sums_ref.shape[0]):
            total = total + sums_ref[s, 0]
        for t in range(tiles):
            own = jnp.concatenate([own_ref[0, t, c] for c in range(children)], axis=1)
            if t > 0:
                total = total + nt(own, own)
            else:
                total = total + jnp.where(q >= PANELS, nt(own, own), 0.0)
        for k in range(PANELS):
            tile = jnp.concatenate([pan_ref[k, 0, 0, c] for c in range(children)], axis=1)
            total = total + nt(tile, tile)
        d_ref[0] = total
        for origin in range(pcol):
            for t in range(tiles):
                if t == 0 and origin < PANELS:
                    continue

                @pl.when((q != origin) & (t * pcol < slot * pcol + q))
                def _():
                    tile = jnp.concatenate(
                        [rowbuf[0, origin, t, c] for c in range(children)], axis=1
                    )
                    d_ref[0] += nt(tile, tile)


def diag(prow, pcol, at, rowbuf, pan, rowtiles, sumbuf, sums, shift):
    cols, _, tiles, children, extent, rank = rowbuf.shape
    kept = rowtiles.shape[0]
    others = sumbuf.shape[0]

    def row(slot, at):
        return (slot * pcol + at[1]) // prow

    return pl.pallas_call(
        functools.partial(diag_kernel, (prow, pcol, kept)),
        out_shape=jax.ShapeDtypeStruct((cols, extent, extent), jnp.float32),
        grid_spec=pltpu.PrefetchScalarGridSpec(
            num_scalar_prefetch=1,
            grid=(cols,),
            in_specs=[
                pl.BlockSpec(
                    (1, pcol, tiles, children, extent, rank), lambda s, at: (s, 0, 0, 0, 0, 0)
                ),
                pl.BlockSpec(
                    (PANELS, 1, 1, children, extent, rank),
                    lambda s, at: (0, row(s, at), 0, 0, 0, 0),
                ),
                pl.BlockSpec(
                    (1, tiles, children, extent, rank), lambda s, at: (row(s, at), 0, 0, 0, 0)
                ),
                pl.BlockSpec((others, 1, extent, extent), lambda s, at: (0, s, 0, 0)),
                pl.BlockSpec((1, extent, extent), lambda s, at: (s, 0, 0)),
                pl.BlockSpec((1, 1, extent), lambda s, at: (s * pcol + at[1], 0, 0)),
            ],
            out_specs=pl.BlockSpec((1, extent, extent), lambda s, at: (s, 0, 0)),
        ),
        compiler_params=pltpu.CompilerParams(vmem_limit_bytes=60 * 2**20),
        cost_estimate=pl.CostEstimate(
            flops=6_000_000_000, bytes_accessed=24 * 2**20, transcendentals=0
        ),
        name="diag",
    )(at, rowbuf, pan, rowtiles, sumbuf, sums, shift)


def finish_kernel(dims, at_ref, rank_ref, u_ref, v_ref, g_ref, h_ref, d_ref, p_ref, o_ref):
    prow, pcol = dims
    r = pl.program_id(0)
    children, cols = u_ref.shape[0], u_ref.shape[3]
    extent, rank_max = u_ref.shape[-2:]
    pieces = extent // STEP
    lane = lax.broadcasted_iota(jnp.int32, (1, rank_max), 1)
    i = r * prow + at_ref[0]

    for t in range(cols):
        j = t * pcol + at_ref[1]

        def put(value, t=t):
            for s in range(pieces):
                o_ref[pl.ds(t * pieces + s, extent, stride=cols * pieces), :] = value[
                    :, s * STEP : (s + 1) * STEP
                ]

        @pl.when(i < j)
        def _():
            put(jnp.zeros((extent, extent), jnp.float32))

        if t == 0:

            @pl.when((i >= j) & (j < PANELS))
            def _():
                put(p_ref[0])

        def total(t=t):
            left, right = [], []
            for c in range(children):
                rank = rank_ref[(c * pl.num_programs(0) + r) * cols + t]
                keep = (lane < rank).astype(jnp.bfloat16)
                left.append(u_ref[c, 0, 0, t, 0])
                right.append(v_ref[c, 0, 0, t, 0] * keep)
            value = nt(jnp.concatenate(left, axis=1), jnp.concatenate(right, axis=1))
            return value - nt(g_ref[0], h_ref[t])

        @pl.when((i > j) & (j >= PANELS))
        def _():
            put(total())

        @pl.when((i == j) & (j >= PANELS))
        def _():
            put(total() + d_ref[t])


def finish(prow, pcol, at, ranks, child_u, child_v, wide, diags, panels):
    children, rows, _, cols, _, extent, rank = child_u.shape
    width = wide.shape[-1]
    lines = extent * cols * extent // STEP
    tile = pl.BlockSpec(
        (children, 1, 1, cols, 1, extent, rank), lambda r, at, ranks: (0, r, 0, 0, 0, 0, 0)
    )
    return pl.pallas_call(
        functools.partial(finish_kernel, (prow, pcol)),
        out_shape=jax.ShapeDtypeStruct((rows * lines, STEP), jnp.float32),
        grid_spec=pltpu.PrefetchScalarGridSpec(
            num_scalar_prefetch=2,
            grid=(rows,),
            in_specs=[
                tile,
                tile,
                pl.BlockSpec((1, extent, width), lambda r, at, ranks: (r, 0, 0)),
                pl.BlockSpec((cols, extent, width), lambda r, at, ranks: (rows // cols, 0, 0)),
                pl.BlockSpec((cols, extent, extent), lambda r, at, ranks: (0, 0, 0)),
                pl.BlockSpec(
                    (1, extent, extent),
                    lambda r, at, ranks: (jnp.where(at[1] < PANELS, r, 0), 0, 0),
                ),
            ],
            out_specs=pl.BlockSpec((lines, STEP), lambda r, at, ranks: (r, 0)),
        ),
        compiler_params=pltpu.CompilerParams(vmem_limit_bytes=56 * 2**20),
        cost_estimate=pl.CostEstimate(
            flops=2 * rows * cols * extent * extent * (width + children * rank),
            bytes_accessed=50 * 2**20,
            transcendentals=0,
        ),
        name="finish",
    )(at, ranks, child_u, child_v, wide, wide, diags, panels)


def on_device(prow, pcol, child_u, child_v, child_rank, diag_shift):
    own_row, own_column = lax.axis_index("prow"), lax.axis_index("pcol")
    children, rows, _, cols, _, extent, rank = child_u.shape
    kept = cols * pcol // prow
    tiles = cols
    at = jnp.stack([own_row, own_column]).astype(jnp.int32)
    ranks = child_rank.reshape(-1)
    shift = diag_shift[:, None, :]
    pan, sums, rowtiles = prep(prow, pcol, kept, tiles, at, ranks, child_u, child_v)
    pan, oth, rowbuf, sumbuf, piv, pair = exchange(prow, pcol, pan, sums, rowtiles)
    lower, inv, car = pivots(piv.reshape(PANELS, extent, extent), shift[:PANELS], pair)
    wide, panels = solve(prow, pcol, at, pan, oth, inv, car, lower)
    diags = diag(prow, pcol, at, rowbuf, pan, rowtiles, sumbuf, sums, shift)
    out = finish(prow, pcol, at, ranks, child_u, child_v, wide, diags, panels)
    return out.reshape(rows, 1, extent, cols, 1, extent)


def solution(mesh):
    placed = (
        P(None, None, "prow", None, "pcol", None, None),
        P(None, None, "prow", None, "pcol", None, None),
        P(None, None, "prow", None, "pcol"),
        P(),
    )
    return jax.shard_map(
        functools.partial(on_device, mesh.shape["prow"], mesh.shape["pcol"]),
        mesh=mesh,
        in_specs=placed,
        out_specs=P(None, "prow", None, None, "pcol", None),
        check_vma=False,
    )
```

time: 1080 us -> 389 us (0.36)
  waiting for transfers between devices: 658 us -> 0 us
  Pallas kernels: 138 us -> 375 us
  matrix products: 106 us -> 0 us
  local copies, waits for them, and re-layouts: 103 us -> 11.8 us
  other arithmetic: 54.6 us -> 0.07 us
  between operations: 14.1 us -> 0.08 us
    psum x6 -> x0, waiting for transfers between devices: 657 us -> none  [the longest x1 270 us: on_device(): panel_factors = lax.psum(jnp.stack(panel_factors), 'pcol')]
    pallas_call x3 -> x6, Pallas kernels: 138 us -> 375 us  [the longest x1 173 us: exchange(): pl.pallas_call(functools.partial(exchange_kernel, (prow, pcol, rows, cols...]
    dot_general x26 -> x0, matrix products: 106 us -> none  [the longest x20 95.1 us: times(): term = jnp.einsum(pattern, a, b, preferred_element_type=jnp.float32)]
    reshape x1, local copies, waits for them, and re-layouts: 30.9 us -> 0.09 us  [on_device(): ranks = child_rank.reshape(-1)]
    gather x4 -> x0, local copies, waits for them, and re-layouts: 24.4 us -> none  [the longest x2 13.2 us: on_device(): scale = jnp.diagonal(lower)]
    select_n x6 -> x0, other arithmetic: 19 us -> none  [the longest x1 10.5 us: on_device(): panels = jnp.where(own_column == k % pcol_count, panel, panels)]
    another operation x3 -> x0, other arithmetic: 12.2 us -> none  [the longest x1 9.18 us: on_device(): panel_factors = lax.psum(jnp.stack(panel_factors), 'pcol')]
    concatenate x3 -> x0, other arithmetic: 11.8 us -> none  [the longest x2 11.8 us: on_device(): wide = jnp.concatenate(rounded, axis=-1)]
  transfers between devices with their start and end apart: 6 -> 0, of which waited for: 6 -> 0; matrix products, arithmetic and copies ran while one was open for 9% -> 0% of each run, Pallas kernels for 10% -> 0%
where the time goes in v1:
time: 389 us; the launch traced here: 387 us
  Pallas kernels  375 us (96%)
  local copies, waits for them, and re-layouts  11.8 us (3%)
    pallas_call x1, Pallas kernels, exchange(): pl.pallas_call(functools.partial(exchange_kernel, (prow, pcol, rows, cols...  173 us
    pallas_call x1, Pallas kernels, pivots(): pl.pallas_call(pivot_kernel, out_shape=(jax.ShapeDtypeStruct((PANELS,) +...  108 us
    pallas_call x1, Pallas kernels, solve(): pl.pallas_call(functools.partial(solve_kernel, (prow, pcol, rows)), out_s...  43.9 us
    pallas_call x1, Pallas kernels, finish(): pl.pallas_call(functools.partial(finish_kernel, (prow, pcol)), out_shape=...  24.3 us
    pallas_call x1, Pallas kernels, diag(): pl.pallas_call(functools.partial(diag_kernel, (prow, pcol, kept)), out_sh...  13.2 us
    pallas_call x1, Pallas kernels, prep(): pl.pallas_call(functools.partial(prep_kernel, (prow, pcol, kept, tiles)),...  12.8 us
    unnamed x23, local copies, waits for them, and re-layouts  9.59 us

profile of v1, /device:TPU:31, one launch (start us, length us, event | category | flops | bytes accessed | tf_op | source)
XLA Modules:
  0.0 387.0 jit_solution(8938356116434785421)
XLA Ops:
  0.0 0.1 pad_add_fusion.at_ref
  0.1 0.7 slice.6
  0.8 0.8 copy.8
  1.6 0.1 reshape.10.rank_ref
  1.7 0.0 copy-start.4
  1.7 1.4 broadcast_in_dim.3.shift_ref
  3.1 2.5 copy-done
  5.6 12.8 %prep.1 = (bf16[2,10,2,2,512,128]{5,4,3,2,1,0:T(8,128)(2,1)}, f32[2,512,512]{2,1,0:T(8,128)S(1)}, bf16[4,2,2,512,128]{4,3,2,1,0:T(8,128)(2,1)S(1)}) custom-call(s32[2]{0:T(128)S(1)} %pad_add_fusion.at_ref, s32[40]{0:T(128)S(1)} %reshape.10.rank_ref, bf16[2,10,1,2,1,512,128]{6,5,4,3,2,1,0:T(8,128)(2,1)S(1)} %copy-done, bf16[2,10,1,2,1,512,128]{6,5,4,3,2,1,0:T(8,128)(2,1)} %v_ref.3), custom_call_target="tpu_custom_call" | custom-call | flops 2684354560 | bytes 18874368 | tf_op jit(solution)/shard_map/prep/pallas_call | solution.py:80
  18.4 0.0 copy-done.3
  18.4 0.0 copy-done.4
  18.4 0.0 copy-start.2
  18.4 172.6 %exchange.1 = (bf16[2,10,2,2,512,128]{5,4,3,2,1,0:T(8,128)(2,1)}, bf16[2,2,2,2,512,128]{5,4,3,2,1,0:T(8,128)(2,1)S(1)}, bf16[2,8,2,2,512,128]{5,4,3,2,1,0:T(8,12...) custom-call(bf16[2,10,2,2,512,128]{5,4,3,2,1,0:T(8,128)(2,1)} %get-t, ...), custom_call_target="tpu_custom_call", output_to_operand_aliasing={{0}: (0, {})} | custom-call | flops 120000004096 | bytes 62914560 | tf_op jit(solution)/shard_map/exchange/pallas_call | solution.py:404
  191.0 0.0 copy-done.1
  191.0 0.0 copy-done.2
  191.0 1.3 copy-done.5
  192.3 1.3 copy-done.7
  193.6 13.2 %diag.1.d_ref = f32[2,512,512]{2,1,0:T(8,128)} custom-call(s32[2]{0:T(128)} %copy-done.3, bf16[2,8,2,2,512,128]{5,4,3,2,1,0:T(8,128)(2,1)} %get-tuple-element.30.rowbuf, bf16[2,10,2,2,512,128]{5,4,3,2,1,0:T(8,128)(2,1)} %get-tuple-element.22.pan_ref, bf16[4,2,2,512,128]{4,3,2,1,0:T(8,128)(2,1)} %copy-done.2, f32[3,2,512,512]{3,2,1,0:T(8,128)} %get-tuple-element.31.sums_ref, ...), custom_call_target="tpu_custom_call" | custom-call | flops 6000000000 | bytes 25165824 | tf_op jit(solution)/shard_map/diag/pallas_call | solution.py:702
  206.8 0.0 copy-done.6
  206.8 108.3 %pivots.1 = (f32[2,512,512]{2,1,0:T(8,128)S(1)}, bf16[2,2,512,512]{3,2,1,0:T(8,128)(2,1)S(1)}, bf16[1,2,512,512]{3,2,1,0:T(8,128)(2,1)S(1)}) custom-call(f32[2,512,512]{2,1,0:T(8,128)S(1)} %bitcast.6, f32[2,1,512]{2,1,0:T(1,128)S(1)} %slice.7.shift_ref, bf16[1,2,2,512,128]{4,3,2,1,0:T(8,128)(2,1)S(1)} %get-tuple-element.25.pair_ref), custom_call_target="tpu_custom_call" | custom-call | flops 99999997952 | bytes 8388608 | tf_op jit(solution)/shard_map/pivots/pallas_call | solution.py:548
  315.2 1.3 copy-done.8
  316.5 1.4 copy-done.9
  317.9 1.0 copy-done.10
  318.8 43.9 %solve.1 = (bf16[12,512,1024]{2,1,0:T(8,128)(2,1)}, f32[10,512,512]{2,1,0:T(8,128)}) custom-call(s32[2]{0:T(128)} %copy-done.3, bf16[2,10,2,2,512,128]{5,4,3,2,1,0:T(8,128)(2,1)} %get-tuple-element.22.pan_ref, bf16[2,2,2,2,512,128]{5,4,3,2,1,0:T(8,128)(2,1)} %copy-done.7, bf16[2,2,512,512]{3,2,1,0:T(8,128)(2,1)} %copy-done.9, ...), custom_call_target="tpu_custom_call" | custom-call | flops 22000001024 | bytes 41943040 | tf_op jit(solution)/shard_map/solve/pallas_call | solution.py:619
  362.7 24.3 %finish.1 = f32[40960,128]{1,0:T(8,128)} custom-call(s32[2]{0:T(128)} %copy-done.3, s32[40]{0:T(128)} %copy-done.4, bf16[2,10,1,2,1,512,128]{6,5,4,3,2,1,0:T(8,128)(2,1)} %u_ref.3, bf16[2,10,1,2,1,512,128]{6,5,4,3,2,1,0:T(8,128)(2,1)} %v_ref.3, bf16[12,512,1024]{2,1,0:T(8,128)(2,1)} %get-tuple-element.29.g_ref.h_ref, ...), custom_call_target="tpu_custom_call" | custom-call | flops 13421772800 | bytes 52428800 | tf_op jit(solution)/shard_map/finish/pallas_call | solution.py:787
  (10 shorter events, 0.0 us)
Async XLA Ops:
  0.1 18.3 %copy-start.3 = (s32[2]{0:T(128)}, s32[2]{0:T(128)S(1)}, u32[]{:S(2)}) copy-start(s32[2]{0:T(128)S(1)} %pad_add_fusion.at_ref) | copy-start | bytes 28
  1.7 16.7 %copy-start.4 = (s32[40]{0:T(128)}, s32[40]{0:T(128)S(1)}, u32[]{:S(2)}) copy-start(s32[40]{0:T(128)S(1)} %reshape.10.rank_ref) | copy-start | bytes 484
  3.1 2.5 copy-start
  18.4 172.6 %copy-start.1 = (f32[2,512,512]{2,1,0:T(8,128)}, f32[2,512,512]{2,1,0:T(8,128)S(1)}, u32[]{:S(2)}) copy-start(f32[2,512,512]{2,1,0:T(8,128)S(1)} %get-tuple-element.20.sum_ref.mine_ref) | copy-start | bytes 6291460
  18.4 172.6 %copy-start.2 = (bf16[4,2,2,512,128]{4,3,2,1,0:T(8,128)(2,1)}, bf16[4,2,2,512,128]{4,3,2,1,0:T(8,128)(2,1)S(1)}, u32[]{:S(2)}) copy-start(bf16[4,2,2,512,128]{4,3,2,1,0:T(8,128)(2,1)S(1)} %get-tuple-element.21.row_ref.own_ref) | copy-start | bytes 6291460
  191.0 1.3 copy-start.5
  192.3 1.3 copy-start.7
  193.6 13.2 %copy-start.6 = (f32[2,4,128,512]{3,2,1,0:T(8,128)S(1)}, f32[2,4,128,512]{3,2,1,0:T(8,128)}, u32[]{:S(2)}) copy-start(f32[2,4,128,512]{3,2,1,0:T(8,128)} %copy-done.5) | copy-start | bytes 6291460
  315.2 1.3 copy-start.8
  316.5 1.4 copy-start.9
  317.8 1.0 copy-start.10

commit v2 on v1

v2 whole, which is shorter than its diff:
```python
import functools

import jax
import jax.numpy as jnp
from jax import lax
from jax.experimental import pallas as pl
from jax.experimental.pallas import tpu as pltpu
from jax.sharding import PartitionSpec as P

PANELS = 2
STEP = 128
SUB = 8
PAIRS = [(m, k) for k in range(PANELS) for m in range(k + 1, PANELS)]
MESH = pl.DeviceIdType.MESH
ANY = pl.BlockSpec(memory_space=pl.ANY)


def nt(a, b, precision=None):
    return lax.dot_general(
        a, b, (((1,), (1,)), ((), ())), preferred_element_type=jnp.float32, precision=precision
    )


def nn(a, b, precision=None):
    return lax.dot_general(
        a, b, (((1,), (0,)), ((), ())), preferred_element_type=jnp.float32, precision=precision
    )


def split(value):
    high = value.astype(jnp.bfloat16)
    low = (value - high.astype(jnp.float32)).astype(jnp.bfloat16)
    return high, low


def prep_kernel(dims, at_ref, rank_ref, u_ref, v_ref, pan_ref, sum_ref, row_ref):
    prow, pcol, kept, tiles = dims
    r = pl.program_id(0)
    children, cols = u_ref.shape[0], u_ref.shape[3]
    rank_max = u_ref.shape[-1]
    lane = lax.broadcasted_iota(jnp.int32, (1, rank_max), 1)

    @pl.when(r == 0)
    def _():
        sum_ref[...] = jnp.zeros_like(sum_ref)

    for t in range(cols):
        left, right = [], []
        for c in range(children):
            rank = rank_ref[(c * pl.num_programs(0) + r) * cols + t]
            keep = (lane < rank).astype(jnp.bfloat16)
            left.append(u_ref[c, 0, 0, t, 0] * keep)
            right.append(v_ref[c, 0, 0, t, 0] * keep)
        if t == 0:
            for c in range(children):
                pan_ref[0, 0, 0, c] = left[c]
                pan_ref[0, 0, 1, c] = right[c]
        if t < tiles:

            @pl.when(r < kept)
            def _(left=left, t=t):
                for c in range(children):
                    row_ref[0, t, c] = left[c]

        wide = jnp.concatenate(right, axis=1)
        sum_ref[t] += nt(wide, wide)
        i = r * prow + at_ref[0]
        j = t * pcol + at_ref[1]

        @pl.when((i == j) & (j < PANELS))
        def _(left=left, wide=wide, t=t):
            sum_ref[t] += nt(jnp.concatenate(left, axis=1), wide)


def prep(prow, pcol, kept, tiles, at, ranks, child_u, child_v):
    children, rows, _, cols, _, extent, rank = child_u.shape
    tile = pl.BlockSpec(
        (children, 1, 1, cols, 1, extent, rank), lambda r, at, ranks: (0, r, 0, 0, 0, 0, 0)
    )
    return pl.pallas_call(
        functools.partial(prep_kernel, (prow, pcol, kept, tiles)),
        out_shape=(
            jax.ShapeDtypeStruct((PANELS, rows, 2, children, extent, rank), jnp.bfloat16),
            jax.ShapeDtypeStruct((cols, extent, extent), jnp.float32),
            jax.ShapeDtypeStruct((kept, tiles, children, extent, rank), jnp.bfloat16),
        ),
        grid_spec=pltpu.PrefetchScalarGridSpec(
            num_scalar_prefetch=2,
            grid=(rows,),
            in_specs=[tile, tile],
            out_specs=(
                pl.BlockSpec(
                    (1, 1, 2, children, extent, rank),
                    lambda r, at, ranks: (lax.rem(at[1], PANELS), r, 0, 0, 0, 0),
                ),
                pl.BlockSpec((cols, extent, extent), lambda r, at, ranks: (0, 0, 0)),
                pl.BlockSpec(
                    (1, tiles, children, extent, rank),
                    lambda r, at, ranks: (jnp.minimum(r, kept - 1), 0, 0, 0, 0),
                ),
            ),
        ),
        compiler_params=pltpu.CompilerParams(vmem_limit_bytes=40 * 2**20),
        cost_estimate=pl.CostEstimate(
            flops=2 * rows * cols * extent * extent * children * rank,
            bytes_accessed=18 * 2**20,
            transcendentals=0,
        ),
        name="prep",
    )(at, ranks, child_u, child_v)


def factor_tile(tile):
    row = lax.broadcasted_iota(jnp.int32, (STEP, STEP), 0)
    lane = lax.broadcasted_iota(jnp.int32, (STEP, STEP), 1)
    left, right = tile, (row == lane).astype(jnp.float32)
    uppers, inverses = [], []
    for base in range(0, STEP, SUB):
        extent = STEP - base
        index = lax.broadcasted_iota(jnp.int32, (extent, STEP), 0)
        weights = [
            jnp.broadcast_to(left[:, base + j : base + j + 1], (extent, STEP)) for j in range(SUB)
        ]
        for j in range(SUB):
            inverse = 1.0 / weights[j][j : j + 1]
            weight = jnp.where(index > j, weights[j], 0.0)
            row_left = left[j : j + 1] * inverse
            row_right = right[j : j + 1] * inverse
            for k in range(j + 1, SUB):
                weights[k] = weights[k] - weight * (weights[k][j : j + 1] * inverse)
            left = left - weight * row_left
            right = right - weight * row_right
        uppers.append(left[:SUB])
        inverses.append(right[:SUB])
        left, right = left[SUB:], right[SUB:]
    return jnp.concatenate(uppers, axis=0), jnp.concatenate(inverses, axis=0)


def factor_block(block, w_ref, e_ref, c_ref, y_ref, between):
    extent = w_ref.shape[0]
    exact = lax.Precision.HIGHEST
    base = pl.multiple_of(block * STEP, STEP)
    here = pl.ds(base, STEP)
    upper, lower_inverse = factor_tile(w_ref[here, here])
    between()
    tile_row = lax.broadcasted_iota(jnp.int32, (STEP, STEP), 0)
    tile_col = lax.broadcasted_iota(jnp.int32, (STEP, STEP), 1)
    pivots = jnp.sum(jnp.where(tile_row == tile_col, upper, 0.0), axis=1, keepdims=True)
    root = jnp.sqrt(pivots)
    pivot_factor = (jnp.where(tile_row <= tile_col, upper, 0.0) / root).T
    pivot_inverse = lower_inverse / root
    panel = nt(w_ref[:, here], pivot_inverse, exact)
    below = lax.broadcasted_iota(jnp.int32, (extent, STEP), 0) >= base + STEP
    panel = jnp.where(below, panel, 0.0)
    c_ref[:, here] = panel
    c_ref[here, here] = pivot_factor
    solved = nn(pivot_inverse, e_ref[here, :], exact)
    y_ref[here, :] = solved
    w_ref[...] -= nt(panel, panel, exact)
    e_ref[...] -= nn(panel, solved, exact)


def exchange_kernel(
    dims, pan_in, sum_ref, row_ref, shift_ref, pan, oth, rowbuf, sumbuf, piv, pair, wide_ref,
    panel_ref, *scratch
):
    prow, pcol, rows, cols, kept, tiles, children = dims
    (part, total, pivots, pairs, w_ref, e_ref, y_ref, c_ref, inv_ref, car_ref, g_ref,
     scale_ref, tile_ref, solved_ref, scaled_ref,
     local, part_s, part_r, sum_s, sum_r, row_s, row_r, chain_s, chain_r, cross_s, cross_r,
     oth_s, oth_r, pair_s, pair_r, gat_s, gat_r, piv_l, pair_l, load_l, store_l, scaled_l) = scratch
    del pan_in
    p, q = lax.axis_index("prow"), lax.axis_index("pcol")
    z, y = q // PANELS, lax.rem(q, PANELS)
    depth = pcol // PANELS
    home = lax.rem(q, prow)
    extent = sum_ref.shape[-1]
    band = extent // prow
    blocks = extent // STEP
    last = 2 * rows
    near = 2 * kept
    early = 4
    turns = PANELS * blocks

    barrier = pltpu.get_barrier_semaphore()
    for d in range(1, pcol):
        pl.semaphore_signal(
            barrier, inc=1, device_id={"pcol": lax.rem(q + d, pcol)}, device_id_type=MESH
        )
    for d in range(1, prow):
        pl.semaphore_signal(
            barrier, inc=1, device_id={"prow": lax.rem(p + d, prow)}, device_id_type=MESH
        )
    pl.semaphore_wait(barrier, pcol + prow - 2)

    def send(src, dst, send_sem, recv_sem, **target):
        return pltpu.make_async_remote_copy(
            src_ref=src, dst_ref=dst, send_sem=send_sem, recv_sem=recv_sem,
            device_id=target, device_id_type=MESH,
        )

    def bands(o):
        return pl.ds(pl.multiple_of(o * band, 8), band)

    def part_copy(d):
        s = lax.rem(p + d, prow)
        return send(
            sum_ref.at[0, bands(s)], part.at[d], part_s.at[d - 1], part_r.at[d - 1], prow=s
        )

    def part_own():
        return pltpu.make_async_copy(sum_ref.at[0, bands(p)], part.at[0], local.at[0])

    def sum_copy():
        d = lax.rem(home + prow - p, prow) - 1
        return send(sum_ref, sumbuf.at[d], sum_s, sum_r.at[d], prow=home)

    def sum_arrival(d):
        return send(sum_ref, sumbuf.at[d], sum_s, sum_r.at[d], prow=home)

    def reach(r):
        return sum(1 for t in range(tiles) if t * pcol < (r + 1) * prow)

    def row_copy(r, first):
        i = r * prow + p
        owner, slot = lax.rem(i, pcol), i // pcol
        window = pl.ds(first, reach(r) - first)
        return send(
            row_ref.at[r, window], rowbuf.at[slot, q, window], row_s.at[r], row_r.at[slot, q],
            pcol=owner,
        )

    def row_arrival(slot, origin, r, first):
        window = pl.ds(first, reach(r) - first)
        return send(
            row_ref.at[r, window], rowbuf.at[slot, origin, window], row_s.at[r],
            row_r.at[slot, origin], pcol=origin,
        )

    def chunk(which, n):
        if isinstance(n, int) and n == last:
            return piv.at[which, bands(p)]
        return pan.at[which, lax.div(n, 2), lax.rem(n, 2)]

    def chain_copy(n):
        ref = chunk(y, n)
        return send(ref, ref, chain_s.at[n], chain_r.at[n], pcol=q + PANELS)

    def cross_copy(n, which):
        ref = chunk(which, n)
        return send(ref, ref, cross_s.at[n], cross_r.at[n], pcol=q + 1 - 2 * y)

    def needed(n, plane):
        if isinstance(n, int) and n == last:
            return plane >= 0
        i = lax.div(n, 2) * prow + p
        used = i >= plane * PANELS
        for m, _ in PAIRS:
            used = used | (i == m)
        return used

    def step(n):
        @pl.when((z > 0) & needed(n, z))
        def _():
            chain_copy(n).wait_recv()

        @pl.when((z < depth - 1) & needed(n, z + 1))
        def _():
            chain_copy(n).start()

        @pl.when(needed(n, z))
        def _():
            cross_copy(n, y).start()

    def cross_arrival(n):
        @pl.when(needed(n, z))
        def _():
            cross_copy(n, 1 - y).wait_recv()

    def oth_row(t):
        return (t * pcol + q) // prow

    def oth_copy(t, k, d):
        n = t * PANELS + k
        return send(
            pan.at[k, oth_row(t)], oth.at[t, k], oth_s.at[n, d - 1], oth_r.at[n],
            prow=lax.rem(p + d, prow),
        )

    def pair_copy(n, d):
        m, k = PAIRS[n]
        return send(
            pan.at[k, m // prow], pair.at[n], pair_s.at[n, d - 1], pair_r.at[n],
            prow=lax.rem(p + d, prow),
        )

    def gat_copy(k, d):
        ref = piv.at[k, bands(p)]
        return send(
            ref, ref, gat_s.at[k, d - 1], gat_r.at[k, d - 1], prow=lax.rem(p + d, prow)
        )

    def gat_arrival(k, d):
        o = lax.rem(p + prow - d, prow)
        ref = piv.at[k, bands(o)]
        return send(ref, ref, gat_s.at[k, d - 1], gat_r.at[k, d - 1], prow=o)

    @pl.when(z == 0)
    def _():
        for d in range(1, prow):
            part_copy(d).start()
        part_own().start()

    step(0)
    step(1)

    @pl.when(z == 0)
    def _():
        part_own().wait()
        for d in range(1, prow):
            part_copy(d).wait_recv()
        value = part[0]
        for d in range(1, prow):
            value = value + part[d]
        total[...] = value
        out = pltpu.make_async_copy(total, piv.at[y, bands(p)], local.at[1])
        out.start()
        out.wait()

    step(last)
    cross_arrival(last)
    for k in range(PANELS):
        for d in range(1, prow):
            gat_copy(k, d).start()

    step(2)
    for n in range(2):
        cross_arrival(n)
    for n, (m, k) in enumerate(PAIRS):

        @pl.when(p == m % prow)
        def _():
            for d in range(1, prow):
                pair_copy(n, d).start()

    @pl.when(p != home)
    def _():
        sum_copy().start()

    for r in range(kept):
        owner = lax.rem(r * prow + p, pcol)

        @pl.when((q != owner) & (z > 0))
        def _():
            row_copy(r, 0).start()

        if reach(r) > 1:

            @pl.when((q != owner) & (z == 0))
            def _():
                row_copy(r, 1).start()

    step(3)
    for k in range(PANELS):
        for d in range(1, prow):
            gat_arrival(k, d).wait_recv()
    loads = [pltpu.make_async_copy(piv.at[k], pivots.at[k], piv_l.at[k]) for k in range(PANELS)]
    for load in loads:
        load.start()
    for load in loads:
        load.wait()

    def near_wait():
        for n in range(2, near):
            cross_arrival(n)

        @pl.when(p == home)
        def _():
            for t in range(cols):
                for k in range(PANELS):
                    for d in range(1, prow):
                        oth_copy(t, k, d).start()

    eye = lax.broadcasted_iota(jnp.int32, (extent, extent), 0) == lax.broadcasted_iota(
        jnp.int32, (extent, extent), 1
    )

    def joined(n, side):
        return jnp.concatenate([pairs[n, side, c] for c in range(children)], axis=1)

    @pl.loop(0, turns)
    def _(turn):
        k, block = lax.div(turn, blocks), lax.rem(turn, blocks)

        @pl.when(block == 0)
        def _():
            w_ref[...] = pivots[k] + jnp.where(eye, shift_ref[pl.ds(k, 1), :], 0.0)
            for n, (m, _) in enumerate(PAIRS):

                @pl.when(k == m)
                def _():
                    left = joined(n, 0)
                    g = g_ref[n]
                    w_ref[...] += nt(left, left) - nt(g, g)

            e_ref[...] = eye.astype(jnp.float32)

        def service():
            @pl.when(turn + early < last)
            def _():
                step(turn + early)

        factor_block(block, w_ref, e_ref, c_ref.at[k], y_ref, service)

        @pl.when(turn == turns - 2)
        def _():
            near_wait()

        @pl.when(turn == blocks - 1)
        def _():
            for n, (m, kk) in enumerate(PAIRS):

                @pl.when(p == m % prow)
                def _():
                    load = pltpu.make_async_copy(pan.at[kk, m // prow], pairs.at[n], pair_l.at[n])
                    load.start()
                    load.wait()

                @pl.when(p != m % prow)
                def _():
                    pair_copy(n, 1).wait_recv()
                    load = pltpu.make_async_copy(pair.at[n], pairs.at[n], pair_l.at[n])
                    load.start()
                    load.wait()

        @pl.when(block == blocks - 1)
        def _():
            high, low = split(y_ref[...])
            inv_ref[k, 0] = high
            inv_ref[k, 1] = low
            scale_ref[k] = jnp.sum(jnp.where(eye, c_ref[k], 0.0), axis=0, keepdims=True)

            for n, (m, kk) in enumerate(PAIRS):

                @pl.when(k == kk)
                def _():
                    right = joined(n, 1)
                    moved = split(nn(high, right) + nn(low, right))
                    left = joined(n, 0)
                    value = nt(left, moved[0]) + nt(left, moved[1])
                    for o, (mo, ko) in enumerate(PAIRS):
                        if mo == m and ko < kk:
                            slot = PAIRS.index((kk, ko))
                            for s in range(2):
                                value = value - nt(g_ref[o], car_ref[slot, s])
                    g_ref[n] = value.astype(jnp.bfloat16)

                @pl.when(k == m)
                def _():
                    g = g_ref[n]
                    one, two = split(nn(high, g) + nn(low, g))
                    car_ref[n, 0] = one
                    car_ref[n, 1] = two

    turn_at = max(rows - 2, kept)
    count = rows + cols
    left_over = max(last - early - turns, 0)
    pace = -(-left_over // rows)

    def is_row(s):
        return (s < turn_at) | (s >= turn_at + cols)

    def row_of(s):
        return jnp.where(s < turn_at, s, s - cols)

    def row_load(s):
        r = row_of(s)
        return pltpu.make_async_copy(
            pan.at[:, r], tile_ref.at[lax.rem(s, 2)], load_l.at[lax.rem(s, 2)]
        )

    def near_load(s):
        t = s - turn_at
        return pltpu.make_async_copy(
            oth.at[t], tile_ref.at[lax.rem(s, 2)], load_l.at[lax.rem(s, 2)]
        )

    def own_load(s, k):
        t = s - turn_at
        return pltpu.make_async_copy(
            pan.at[k, oth_row(t)], tile_ref.at[lax.rem(s, 2), k],
            local.at[2 + t * PANELS + k],
        )

    def begin(s):
        @pl.when(is_row(s))
        def _():
            r = row_of(s)

            @pl.when(r >= kept)
            def _():
                cross_arrival(2 * r)
                cross_arrival(2 * r + 1)

            row_load(s).start()

        @pl.when(jnp.logical_not(is_row(s)))
        def _():
            @pl.when(p == home)
            def _():
                for k in range(PANELS):
                    own_load(s, k).start()

            @pl.when(p != home)
            def _():
                for k in range(PANELS):
                    n = (s - turn_at) * PANELS + k
                    send(
                        oth.at[s - turn_at, k], oth.at[s - turn_at, k], oth_s.at[n, 0],
                        oth_r.at[n], prow=home,
                    ).wait_recv()
                near_load(s).start()

    def ready(s):
        @pl.when(is_row(s))
        def _():
            row_load(s).wait()

        @pl.when(jnp.logical_not(is_row(s)) & (p == home))
        def _():
            for k in range(PANELS):
                own_load(s, k).wait()

        @pl.when(jnp.logical_not(is_row(s)) & (p != home))
        def _():
            near_load(s).wait()

    def store(s):
        place = jnp.where(is_row(s), row_of(s), rows + s - turn_at)
        return pltpu.make_async_copy(
            solved_ref.at[lax.rem(s, 2)], wide_ref.at[place], store_l.at[lax.rem(s, 2)]
        )

    def scaled_store(s):
        return pltpu.make_async_copy(
            scaled_ref.at[lax.rem(s, 2)], panel_ref.at[row_of(s)], scaled_l.at[lax.rem(s, 2)]
        )

    begin(0)

    @pl.loop(0, count)
    def _(s):
        for c in range(pace):
            n = early + turns + pace * s + c

            @pl.when(n < last)
            def _(n=n):
                step(n)

        @pl.when(s + 1 < count)
        def _():
            begin(s + 1)

        ready(s)

        @pl.when(s >= 2)
        def _():
            store(s - 2).wait()

            @pl.when(is_row(s - 2) & (q < PANELS))
            def _():
                scaled_store(s - 2).wait()

        slot = lax.rem(s, 2)
        index = jnp.where(is_row(s), row_of(s) * prow + p, (s - turn_at) * pcol + q)
        solved = []
        for k in range(PANELS):
            left = jnp.concatenate([tile_ref[slot, k, 0, c] for c in range(children)], axis=1)
            right = jnp.concatenate([tile_ref[slot, k, 1, c] for c in range(children)], axis=1)
            moved = split(nn(inv_ref[k, 0], right) + nn(inv_ref[k, 1], right))
            value = nt(left, moved[0]) + nt(left, moved[1])
            for kk in range(k):
                pos = PAIRS.index((k, kk))
                value = value - nt(solved[kk], car_ref[pos, 0]) - nt(solved[kk], car_ref[pos, 1])
            value = jnp.where(index > k, value, 0.0)
            solved.append(value.astype(jnp.bfloat16))
            solved_ref[slot, :, k * extent : (k + 1) * extent] = solved[k]

            @pl.when((q == k) & is_row(s))
            def _(value=value, k=k):
                scaled_ref[slot] = jnp.where(index == k, c_ref[k], value) * scale_ref[k]

        store(s).start()

        @pl.when(is_row(s) & (q < PANELS))
        def _():
            scaled_store(s).start()

    for s in range(count - 2, count):
        store(s).wait()

        @pl.when(is_row(s) & (q < PANELS))
        def _():
            scaled_store(s).wait()

    for k in range(PANELS):
        for d in range(1, prow):
            gat_copy(k, d).wait_send()
    for n, (m, k) in enumerate(PAIRS):

        @pl.when(p == m % prow)
        def _():
            for d in range(1, prow):
                pair_copy(n, d).wait_send()

    @pl.when(p == home)
    def _():
        for t in range(cols):
            for k in range(PANELS):
                for d in range(1, prow):
                    oth_copy(t, k, d).wait_send()
        for d in range(prow - 1):
            sum_arrival(d).wait_recv()
        for slot in range(cols):
            for origin in range(pcol):

                @pl.when(q != origin)
                def _():
                    low = slot * pcol // prow
                    first = 1 if origin < PANELS else 0
                    if reach(low) > first:
                        row_arrival(slot, origin, low, first).wait_recv()

    @pl.when(p != home)
    def _():
        sum_copy().wait_send()

    @pl.when(z == 0)
    def _():
        for d in range(1, prow):
            part_copy(d).wait_send()

    for r in range(kept):
        owner = lax.rem(r * prow + p, pcol)

        @pl.when((q != owner) & (z > 0))
        def _():
            row_copy(r, 0).wait_send()

        if reach(r) > 1:

            @pl.when((q != owner) & (z == 0))
            def _():
                row_copy(r, 1).wait_send()

    for n in range(last + 1):

        @pl.when((z < depth - 1) & needed(n, z + 1))
        def _():
            chain_copy(n).wait_send()

        @pl.when(needed(n, z))
        def _():
            cross_copy(n, y).wait_send()


def exchange(prow, pcol, pan, sums, rowtiles, shift):
    _, rows, _, children, extent, rank = pan.shape
    cols = sums.shape[0]
    kept, tiles = rowtiles.shape[:2]
    band = extent // prow
    pairs = max(len(PAIRS), 1)
    dma = pltpu.SemaphoreType.DMA
    square = (extent, extent)
    narrow = pan.dtype
    return pl.pallas_call(
        functools.partial(exchange_kernel, (prow, pcol, rows, cols, kept, tiles, children)),
        out_shape=(
            jax.ShapeDtypeStruct(pan.shape, narrow),
            jax.ShapeDtypeStruct((cols, PANELS, 2, children, extent, rank), narrow),
            jax.ShapeDtypeStruct((cols, pcol, tiles, children, extent, rank), narrow),
            jax.ShapeDtypeStruct((prow - 1, cols) + square, jnp.float32),
            jax.ShapeDtypeStruct((PANELS,) + square, jnp.float32),
            jax.ShapeDtypeStruct((pairs, 2, children, extent, rank), narrow),
            jax.ShapeDtypeStruct((rows + cols, extent, PANELS * extent), narrow),
            jax.ShapeDtypeStruct((rows,) + square, jnp.float32),
        ),
        in_specs=[ANY, ANY, ANY, pl.BlockSpec(memory_space=pltpu.VMEM)],
        out_specs=(ANY,) * 8,
        scratch_shapes=[
            pltpu.VMEM((prow, band, extent), jnp.float32),
            pltpu.VMEM((band, extent), jnp.float32),
            pltpu.VMEM((PANELS,) + square, jnp.float32),
            pltpu.VMEM((pairs, 2, children, extent, rank), narrow),
            pltpu.VMEM(square, jnp.float32),
            pltpu.VMEM(square, jnp.float32),
            pltpu.VMEM(square, jnp.float32),
            pltpu.VMEM((PANELS,) + square, jnp.float32),
            pltpu.VMEM((PANELS, 2) + square, narrow),
            pltpu.VMEM((pairs, 2) + square, narrow),
            pltpu.VMEM((pairs,) + square, narrow),
            pltpu.VMEM((PANELS, 1, extent), jnp.float32),
            pltpu.VMEM((2, PANELS, 2, children, extent, rank), narrow),
            pltpu.VMEM((2, extent, PANELS * extent), narrow),
            pltpu.VMEM((2,) + square, jnp.float32),
            dma((2 + cols * PANELS,)),
            dma((prow - 1,)),
            dma((prow - 1,)),
            dma,
            dma((prow - 1,)),
            dma((kept,)),
            dma((cols, pcol)),
            dma((2 * rows + 1,)),
            dma((2 * rows + 1,)),
            dma((2 * rows + 1,)),
            dma((2 * rows + 1,)),
            dma((cols * PANELS, prow - 1)),
            dma((cols * PANELS,)),
            dma((pairs, prow - 1)),
            dma((pairs,)),
            dma((PANELS, prow - 1)),
            dma((PANELS, prow - 1)),
            dma((PANELS,)),
            dma((pairs,)),
            dma((2,)),
            dma((2,)),
            dma((2,)),
        ],
        input_output_aliases={0: 0},
        compiler_params=pltpu.CompilerParams(
            collective_id=0, has_side_effects=True, vmem_limit_bytes=67_043_328
        ),
        cost_estimate=pl.CostEstimate(
            flops=120_000_000_000, bytes_accessed=90 * 2**20, transcendentals=0
        ),
        name="exchange",
    )(pan, sums, rowtiles, shift)


def diag_kernel(dims, at_ref, rowbuf, pan_ref, own_ref, sums_ref, mine_ref, shift_ref, d_ref):
    prow, pcol, kept = dims
    slot = pl.program_id(0)
    tiles, children, extent = rowbuf.shape[2], rowbuf.shape[3], rowbuf.shape[4]
    q = at_ref[1]

    @pl.when(at_ref[0] == lax.rem(q, prow))
    def _():
        eye = lax.broadcasted_iota(jnp.int32, (extent, extent), 0) == lax.broadcasted_iota(
            jnp.int32, (extent, extent), 1
        )
        shift = shift_ref[pl.ds(slot * pcol + q, 1), :]
        total = mine_ref[0] + jnp.where(eye, shift, 0.0)
        for s in range(sums_ref.shape[0]):
            total = total + sums_ref[s, 0]
        for t in range(tiles):
            own = jnp.concatenate([own_ref[0, t, c] for c in range(children)], axis=1)
            if t > 0:
                total = total + nt(own, own)
            else:
                total = total + jnp.where(q >= PANELS, nt(own, own), 0.0)
        for k in range(PANELS):
            tile = jnp.concatenate([pan_ref[k, 0, 0, c] for c in range(children)], axis=1)
            total = total + nt(tile, tile)
        d_ref[0] = total
        for origin in range(pcol):
            for t in range(tiles):
                if t == 0 and origin < PANELS:
                    continue

                @pl.when((q != origin) & (t * pcol < slot * pcol + q))
                def _():
                    tile = jnp.concatenate(
                        [rowbuf[0, origin, t, c] for c in range(children)], axis=1
                    )
                    d_ref[0] += nt(tile, tile)


def diag(prow, pcol, at, rowbuf, pan, rowtiles, sumbuf, sums, shift):
    cols, _, tiles, children, extent, rank = rowbuf.shape
    kept = rowtiles.shape[0]
    others = sumbuf.shape[0]

    def row(slot, at):
        return (slot * pcol + at[1]) // prow

    return pl.pallas_call(
        functools.partial(diag_kernel, (prow, pcol, kept)),
        out_shape=jax.ShapeDtypeStruct((cols, extent, extent), jnp.float32),
        grid_spec=pltpu.PrefetchScalarGridSpec(
            num_scalar_prefetch=1,
            grid=(cols,),
            in_specs=[
                pl.BlockSpec(
                    (1, pcol, tiles, children, extent, rank), lambda s, at: (s, 0, 0, 0, 0, 0)
                ),
                pl.BlockSpec(
                    (PANELS, 1, 1, children, extent, rank),
                    lambda s, at: (0, row(s, at), 0, 0, 0, 0),
                ),
                pl.BlockSpec(
                    (1, tiles, children, extent, rank), lambda s, at: (row(s, at), 0, 0, 0, 0)
                ),
                pl.BlockSpec((others, 1, extent, extent), lambda s, at: (0, s, 0, 0)),
                pl.BlockSpec((1, extent, extent), lambda s, at: (s, 0, 0)),
                pl.BlockSpec(shift.shape, lambda s, at: (0, 0)),
            ],
            out_specs=pl.BlockSpec((1, extent, extent), lambda s, at: (s, 0, 0)),
        ),
        compiler_params=pltpu.CompilerParams(vmem_limit_bytes=60 * 2**20),
        cost_estimate=pl.CostEstimate(
            flops=6_000_000_000, bytes_accessed=24 * 2**20, transcendentals=0
        ),
        name="diag",
    )(at, rowbuf, pan, rowtiles, sumbuf, sums, shift)


def finish_kernel(dims, at_ref, rank_ref, u_ref, v_ref, g_ref, h_ref, d_ref, p_ref, o_ref):
    prow, pcol = dims
    r = pl.program_id(0)
    children, cols = u_ref.shape[0], u_ref.shape[3]
    extent, rank_max = u_ref.shape[-2:]
    pieces = extent // STEP
    lane = lax.broadcasted_iota(jnp.int32, (1, rank_max), 1)
    i = r * prow + at_ref[0]

    for t in range(cols):
        j = t * pcol + at_ref[1]

        def put(value, t=t):
            for s in range(pieces):
                o_ref[pl.ds(t * pieces + s, extent, stride=cols * pieces), :] = value[
                    :, s * STEP : (s + 1) * STEP
                ]

        @pl.when(i < j)
        def _():
            put(jnp.zeros((extent, extent), jnp.float32))

        if t == 0:

            @pl.when((i >= j) & (j < PANELS))
            def _():
                put(p_ref[0])

        def total(t=t):
            left, right = [], []
            for c in range(children):
                rank = rank_ref[(c * pl.num_programs(0) + r) * cols + t]
                keep = (lane < rank).astype(jnp.bfloat16)
                left.append(u_ref[c, 0, 0, t, 0])
                right.append(v_ref[c, 0, 0, t, 0] * keep)
            value = nt(jnp.concatenate(left, axis=1), jnp.concatenate(right, axis=1))
            return value - nt(g_ref[0], h_ref[t])

        @pl.when((i > j) & (j >= PANELS))
        def _():
            put(total())

        @pl.when((i == j) & (j >= PANELS))
        def _():
            put(total() + d_ref[t])


def finish(prow, pcol, at, ranks, child_u, child_v, wide, diags, panels):
    children, rows, _, cols, _, extent, rank = child_u.shape
    width = wide.shape[-1]
    lines = extent * cols * extent // STEP
    tile = pl.BlockSpec(
        (children, 1, 1, cols, 1, extent, rank), lambda r, at, ranks: (0, r, 0, 0, 0, 0, 0)
    )
    return pl.pallas_call(
        functools.partial(finish_kernel, (prow, pcol)),
        out_shape=jax.ShapeDtypeStruct((rows * lines, STEP), jnp.float32),
        grid_spec=pltpu.PrefetchScalarGridSpec(
            num_scalar_prefetch=2,
            grid=(rows,),
            in_specs=[
                tile,
                tile,
                pl.BlockSpec((1, extent, width), lambda r, at, ranks: (r, 0, 0)),
                pl.BlockSpec((cols, extent, width), lambda r, at, ranks: (rows // cols, 0, 0)),
                pl.BlockSpec((cols, extent, extent), lambda r, at, ranks: (0, 0, 0)),
                pl.BlockSpec(
                    (1, extent, extent),
                    lambda r, at, ranks: (jnp.where(at[1] < PANELS, r, 0), 0, 0),
                ),
            ],
            out_specs=pl.BlockSpec((lines, STEP), lambda r, at, ranks: (r, 0)),
        ),
        compiler_params=pltpu.CompilerParams(vmem_limit_bytes=56 * 2**20),
        cost_estimate=pl.CostEstimate(
            flops=2 * rows * cols * extent * extent * (width + children * rank),
            bytes_accessed=50 * 2**20,
            transcendentals=0,
        ),
        name="finish",
    )(at, ranks, child_u, child_v, wide, wide, diags, panels)


def on_device(prow, pcol, child_u, child_v, child_rank, diag_shift):
    own_row, own_column = lax.axis_index("prow"), lax.axis_index("pcol")
    children, rows, _, cols, _, extent, rank = child_u.shape
    kept = cols * pcol // prow
    tiles = cols
    at = jnp.stack([own_row, own_column]).astype(jnp.int32)
    ranks = child_rank.reshape(-1)
    pan, sums, rowtiles = prep(prow, pcol, kept, tiles, at, ranks, child_u, child_v)
    pan, _, rowbuf, sumbuf, _, _, wide, panels = exchange(
        prow, pcol, pan, sums, rowtiles, diag_shift
    )
    diags = diag(prow, pcol, at, rowbuf, pan, rowtiles, sumbuf, sums, diag_shift)
    out = finish(prow, pcol, at, ranks, child_u, child_v, wide, diags, panels)
    return out.reshape(rows, 1, extent, cols, 1, extent)


def solution(mesh):
    placed = (
        P(None, None, "prow", None, "pcol", None, None),
        P(None, None, "prow", None, "pcol", None, None),
        P(None, None, "prow", None, "pcol"),
        P(),
    )
    return jax.shard_map(
        functools.partial(on_device, mesh.shape["prow"], mesh.shape["pcol"]),
        mesh=mesh,
        in_specs=placed,
        out_specs=P(None, "prow", None, None, "pcol", None),
        check_vma=False,
    )
```

time: 389 us -> 256 us (0.66)
  Pallas kernels: 375 us -> 249 us
  local copies, waits for them, and re-layouts: 11.8 us -> 5.97 us
    pallas_call x2 -> x0, Pallas kernels: 152 us -> none  [the longest x1 108 us: pivots(): pl.pallas_call(pivot_kernel, out_shape=(jax.ShapeDtypeStruct((PANELS,) +...]
    pallas_call x1, Pallas kernels: 173 us -> 199 us  [exchange(): pl.pallas_call(functools.partial(exchange_kernel, (prow, pcol, rows, cols...]
    unnamed x23 -> x11, local copies, waits for them, and re-layouts: 9.59 us -> 5.88 us
where the time goes in v2:
time: 256 us; the launch traced here: 255 us
  Pallas kernels  249 us (97%)
  local copies, waits for them, and re-layouts  5.97 us (2%)
    pallas_call x1, Pallas kernels, exchange(): pl.pallas_call(functools.partial(exchange_kernel, (prow, pcol, rows, cols...  199 us
    pallas_call x1, Pallas kernels, finish(): pl.pallas_call(functools.partial(finish_kernel, (prow, pcol)), out_shape=...  24.3 us
    pallas_call x1, Pallas kernels, diag(): pl.pallas_call(functools.partial(diag_kernel, (prow, pcol, kept)), out_sh...  13.1 us
    pallas_call x1, Pallas kernels, prep(): pl.pallas_call(functools.partial(prep_kernel, (prow, pcol, kept, tiles)),...  12.8 us
    unnamed x11, local copies, waits for them, and re-layouts  5.88 us

profile of v2, /device:TPU:31, one launch (start us, length us, event | category | flops | bytes accessed | tf_op | source)
XLA Modules:
  0.0 255.3 jit_solution(12039006922586909414)
XLA Ops:
  0.0 0.1 pad_add_fusion.at_ref
  0.1 0.0 copy-start.3
  0.1 0.8 copy.8
  0.9 0.1 reshape.6.rank_ref
  0.9 0.0 copy-start
  1.0 2.5 copy-done
  3.4 0.0 copy-start.4
  3.4 12.8 %prep.1 = (bf16[2,10,2,2,512,128]{5,4,3,2,1,0:T(8,128)(2,1)}, f32[2,512,512]{2,1,0:T(8,128)S(1)}, bf16[4,2,2,512,128]{4,3,2,1,0:T(8,128)(2,1)S(1)}) custom-call(s32[2]{0:T(128)S(1)} %pad_add_fusion.at_ref, s32[40]{0:T(128)S(1)} %reshape.6.rank_ref, bf16[2,10,1,2,1,512,128]{6,5,4,3,2,1,0:T(8,128)(2,1)S(1)} %copy-done, bf16[2,10,1,2,1,512,128]{6,5,4,3,2,1,0:T(8,128)(2,1)} %v_ref.3), custom_call_target="tpu_custom_call" | custom-call | flops 2684354560 | bytes 18874368 | tf_op jit(solution)/shard_map/prep/pallas_call | solution.py:80
  16.3 0.0 copy-done.3
  16.3 0.0 copy-start.1
  16.3 1.3 copy-done.1
  17.6 0.0 copy-start.2
  17.6 1.3 copy-done.2
  18.9 0.0 copy-done.4
  18.9 199.0 %exchange.1 = (bf16[2,10,2,2,512,128]{5,4,3,2,1,0:T(8,128)(2,1)}, bf16[2,2,2,2,512,128]{5,4,3,2,1,0:T(8,128)(2,1)}, bf16[2,8,2,2,512,128]{5,4,3,2,1,0:T(8,128)(2...) custom-call(bf16[2,10,2,2,512,128]{5,4,3,2,1,0:T(8,128)(2,1)} %get-t, ...), custom_call_target="tpu_custom_call", output_to_operand_aliasing={{0}: (0, {})} | custom-call | flops 120000004096 | bytes 94371840 | tf_op jit(solution)/shard_map/exchange/pallas_call | solution.py:676
  217.9 13.1 %diag.1.d_ref = f32[2,512,512]{2,1,0:T(8,128)} custom-call(s32[2]{0:T(128)} %copy-done.3, bf16[2,8,2,2,512,128]{5,4,3,2,1,0:T(8,128)(2,1)} %get-tuple-element.17.rowbuf, bf16[2,10,2,2,512,128]{5,4,3,2,1,0:T(8,128)(2,1)} %get-tuple-element.18.pan_ref, bf16[4,2,2,512,128]{4,3,2,1,0:T(8,128)(2,1)} %copy-done.2, f32[3,2,512,512]{3,2,1,0:T(8,128)} %get-tuple-element.19.sums_ref, ...), custom_call_target="tpu_custom_call" | custom-call | flops 6000000000 | bytes 25165824 | tf_op jit(solution)/shard_map/diag/pallas_call | solution.py:786
  231.0 24.3 %finish.1 = f32[40960,128]{1,0:T(8,128)} custom-call(s32[2]{0:T(128)} %copy-done.3, s32[40]{0:T(128)} %copy-done.4, bf16[2,10,1,2,1,512,128]{6,5,4,3,2,1,0:T(8,128)(2,1)} %u_ref.3, bf16[2,10,1,2,1,512,128]{6,5,4,3,2,1,0:T(8,128)(2,1)} %v_ref.3, bf16[12,512,1024]{2,1,0:T(8,128)(2,1)} %get-tuple-element.16.g_ref.h_ref, ...), custom_call_target="tpu_custom_call" | custom-call | flops 13421772800 | bytes 52428800 | tf_op jit(solution)/shard_map/finish/pallas_call | solution.py:871
Async XLA Ops:
  0.1 16.2 %copy-start.3 = (s32[2]{0:T(128)}, s32[2]{0:T(128)S(1)}, u32[]{:S(2)}) copy-start(s32[2]{0:T(128)S(1)} %pad_add_fusion.at_ref) | copy-start | bytes 28
  0.9 2.5 copy-start
  3.4 15.4 %copy-start.4 = (s32[40]{0:T(128)}, s32[40]{0:T(128)S(1)}, u32[]{:S(2)}) copy-start(s32[40]{0:T(128)S(1)} %reshape.6.rank_ref) | copy-start | bytes 484
  16.3 1.3 copy-start.1
  17.6 1.3 copy-start.2

commit v3 on v2

--- a/solution.py
+++ b/solution.py
@@ -100,7 +100,7 @@
                 ),
             ),
         ),
-        compiler_params=pltpu.CompilerParams(vmem_limit_bytes=40 * 2**20),
+        compiler_params=pltpu.CompilerParams(vmem_limit_bytes=67_043_328),
         cost_estimate=pl.CostEstimate(
             flops=2 * rows * cols * extent * extent * children * rank,
             bytes_accessed=18 * 2**20,
@@ -311,8 +311,14 @@
             part_copy(d).start()
         part_own().start()
 
+    for r in range(kept):
+        owner = lax.rem(r * prow + p, pcol)
+
+        @pl.when((q != owner) & (z > 0))
+        def _():
+            row_copy(r, 0).start()
+
     step(0)
-    step(1)
 
     @pl.when(z == 0)
     def _():
@@ -333,6 +339,7 @@
         for d in range(1, prow):
             gat_copy(k, d).start()
 
+    step(1)
     step(2)
     for n in range(2):
         cross_arrival(n)
@@ -349,11 +356,6 @@
 
     for r in range(kept):
         owner = lax.rem(r * prow + p, pcol)
-
-        @pl.when((q != owner) & (z > 0))
-        def _():
-            row_copy(r, 0).start()
-
         if reach(r) > 1:
 
             @pl.when((q != owner) & (z == 0))
@@ -412,7 +414,7 @@
 
         factor_block(block, w_ref, e_ref, c_ref.at[k], y_ref, service)
 
-        @pl.when(turn == turns - 2)
+        @pl.when(turn == turns - 3)
         def _():
             near_wait()
 
@@ -806,7 +808,7 @@
             ],
             out_specs=pl.BlockSpec((1, extent, extent), lambda s, at: (s, 0, 0)),
         ),
-        compiler_params=pltpu.CompilerParams(vmem_limit_bytes=60 * 2**20),
+        compiler_params=pltpu.CompilerParams(vmem_limit_bytes=67_043_328),
         cost_estimate=pl.CostEstimate(
             flops=6_000_000_000, bytes_accessed=24 * 2**20, transcendentals=0
         ),
@@ -887,7 +889,7 @@
             ],
             out_specs=pl.BlockSpec((lines, STEP), lambda r, at, ranks: (r, 0)),
         ),
-        compiler_params=pltpu.CompilerParams(vmem_limit_bytes=56 * 2**20),
+        compiler_params=pltpu.CompilerParams(vmem_limit_bytes=67_043_328),
         cost_estimate=pl.CostEstimate(
             flops=2 * rows * cols * extent * extent * (width + children * rank),
             bytes_accessed=50 * 2**20,

time: 256 us -> 243 us (0.949); the launches traced: 255 us -> 239 us
  Pallas kernels: 249 us -> 237 us
  local copies, waits for them, and re-layouts: 5.97 us -> 1.45 us
    pallas_call x1, Pallas kernels: 199 us -> 185 us  [exchange(): pl.pallas_call(functools.partial(exchange_kernel, (prow, pcol, rows, cols...]
    unnamed x11 -> x1, local copies, waits for them, and re-layouts: 5.88 us -> 0.78 us
where the time goes in v3:
time: 243 us; the launch traced here: 239 us
  Pallas kernels  237 us (98%)
    pallas_call x1, Pallas kernels, exchange(): pl.pallas_call(functools.partial(exchange_kernel, (prow, pcol, rows, cols...  185 us
    pallas_call x1, Pallas kernels, finish(): pl.pallas_call(functools.partial(finish_kernel, (prow, pcol)), out_shape=...  24.3 us
    pallas_call x1, Pallas kernels, prep(): pl.pallas_call(functools.partial(prep_kernel, (prow, pcol, kept, tiles)),...  14.9 us
    pallas_call x1, Pallas kernels, diag(): pl.pallas_call(functools.partial(diag_kernel, (prow, pcol, kept)), out_sh...  13.1 us

profile of v3, /device:TPU:31, one launch (start us, length us, event | category | flops | bytes accessed | tf_op | source)
XLA Modules:
  0.0 238.9 jit_solution(8497196239505263971)
XLA Ops:
  0.0 0.6 pad_add_fusion.at_ref
  0.6 0.8 copy.8
  1.4 0.7 reshape.6.rank_ref
  2.1 14.9 %prep.1 = (bf16[2,10,2,2,512,128]{5,4,3,2,1,0:T(8,128)(2,1)}, f32[2,512,512]{2,1,0:T(8,128)}, bf16[4,2,2,512,128]{4,3,2,1,0:T(8,128)(2,1)}) custom-call(s32[2]{0:T(128)} %pad_add_fusion.at_ref, s32[40]{0:T(128)} %reshape.6.rank_ref, bf16[2,10,1,2,1,512,128]{6,5,4,3,2,1,0:T(8,128)(2,1)} %u_ref.3, bf16[2,10,1,2,1,512,128]{6,5,4,3,2,1,0:T(8,128)(2,1)} %v_ref.3), custom_call_target="tpu_custom_call" | custom-call | flops 2684354560 | bytes 18874368 | tf_op jit(solution)/shard_map/prep/pallas_call | solution.py:80
  17.0 184.6 %exchange.1 = (bf16[2,10,2,2,512,128]{5,4,3,2,1,0:T(8,128)(2,1)}, bf16[2,2,2,2,512,128]{5,4,3,2,1,0:T(8,128)(2,1)}, bf16[2,8,2,2,512,128]{5,4,3,2,1,0:T(8,128)(2...) custom-call(bf16[2,10,2,2,512,128]{5,4,3,2,1,0:T(8,128)(2,1)} %get-t, ...), custom_call_target="tpu_custom_call", output_to_operand_aliasing={{0}: (0, {})} | custom-call | flops 120000004096 | bytes 94371840 | tf_op jit(solution)/shard_map/exchange/pallas_call | solution.py:678
  201.5 13.1 %diag.1.d_ref = f32[2,512,512]{2,1,0:T(8,128)} custom-call(s32[2]{0:T(128)} %pad_add_fusion.at_ref, bf16[2,8,2,2,512,128]{5,4,3,2,1,0:T(8,128)(2,1)} %get-tuple-element.17.rowbuf, bf16[2,10,2,2,512,128]{5,4,3,2,1,0:T(8,128)(2,1)} %get-tuple-element.18.pan_ref, bf16[4,2,2,512,128]{4,3,2,1,0:T(8,128)(2,1)} %get-tuple-element.15.row_ref.own_ref, ...), custom_call_target="tpu_custom_call" | custom-call | flops 6000000000 | bytes 25165824 | tf_op jit(solution)/shard_map/diag/pallas_call | solution.py:788
  214.6 24.3 %finish.1 = f32[40960,128]{1,0:T(8,128)} custom-call(s32[2]{0:T(128)} %pad_add_fusion.at_ref, s32[40]{0:T(128)} %reshape.6.rank_ref, bf16[2,10,1,2,1,512,128]{6,5,4,3,2,1,0:T(8,128)(2,1)} %u_ref.3, bf16[2,10,1,2,1,512,128]{6,5,4,3,2,1,0:T(8,128)(2,1)} %v_ref.3, bf16[12,512,1024]{2,1,0:T(8,128)(2,1)} %get-tuple-element.16.g_ref.h_ref, ...), custom_call_target="tpu_custom_call" | custom-call | flops 13421772800 | bytes 52428800 | tf_op jit(solution)/shard_map/finish/pallas_call | solution.py:873
